TPU v7x, 256 devices: a whole 4x4x8 slice. The times are simulated.
256 devices in a mesh: level: 2 (over core), gx: 4 (over x), yz: 32 (over z, y).
Axes of the slice: x: 4, y: 4, z: 8, core: 2. Of those that a mesh axis runs over, the one named last changes fastest.
Arguments:
- init_field: float32 [128, 512, 256], P('gx', 'yz'), may hold values from -6 to 6
- source: float32 [128, 512, 256], P('gx', 'yz'), may hold values from -4 to 4
- damping: float32 [128, 512, 256], P('gx', 'yz'), may hold values from 0.05 to 2
Outputs:
- final_states: float32 [2, 128, 512, 256], P('level', 'gx', 'yz')
All inputs are finite; a program needn't handle non-finite values.
Results may differ from a plain program's by a relative error of at most 0.0001.
Values sent between devices are 32-bit elements; how exact they have to be, the bound alone decides.
A program may use at most 64 MiB of HBM per device.

v0:
```python
import functools

import jax
import jax.numpy as jnp
from jax import lax
from jax.sharding import Mesh
from jax.sharding import PartitionSpec as P

STEPS = 3
ITERS = 3
GX_YZ = ("gx", "yz_0", "yz_1")
YZ = ("yz_0", "yz_1")


diffusion_number = 1.0


def padded_2(shard, sides, width):
    edges = {}
    for axis, dim in sides:
        size, length = (lax.axis_size(axis), shard.shape[dim])
        up = [(i, (i + 1) % size) for i in range(size - 1)]
        last = lax.slice_in_dim(shard, length - width, length, axis=dim)
        initial = lax.slice_in_dim(shard, 0, width, axis=dim)
        edges[dim] = (
            lax.ppermute(last, axis, up),
            lax.ppermute(initial, axis, [(b, a) for a, b in up]),
        )
    done = []
    for _, dim in sides:
        low, high = edges[dim]
        around = [(width, width) if d in done else (0, 0) for d in range(shard.ndim)]
        shard = jnp.concatenate([jnp.pad(low, around), shard, jnp.pad(high, around)], axis=dim)
        done.append(dim)
    return shard


def one_axis_at_a_time(shard, axes):
    return functools.reduce(lax.psum, axes, shard)


def passed_along(block, axis, distance):
    devices = range(lax.axis_size(axis))
    route = [(i - distance, i) for i in devices if i - distance in devices]
    return lax.ppermute(block, axis, route)


def stencil_from(padded, field, damping):
    beside = padded[2:, 1:-1, :] + padded[:-2, 1:-1, :]
    beside = beside + padded[1:-1, 2:, :] + padded[1:-1, :-2, :]
    zero_plane = jnp.zeros_like(field[:, :, :1])
    beside = beside + jnp.concatenate([field[:, :, 1:], zero_plane], axis=2)
    beside = beside + jnp.concatenate([zero_plane, field[:, :, :-1]], axis=2)
    return damping * field + diffusion_number * (6.0 * field - beside)


def operate(field, damping):
    padded = padded_2(field, (("gx", 0), (YZ, 1)), 1)
    return field + stencil_from(padded, field, damping)


def two_products(resid, image):
    return (
        one_axis_at_a_time(jnp.sum(resid * resid), GX_YZ),
        one_axis_at_a_time(jnp.sum(resid * image), GX_YZ),
    )


def solve(target, guess, damping):
    answer = guess
    resid = target - operate(answer, damping)
    image = operate(resid, damping)
    norm_now, product = two_products(resid, image)
    alpha = norm_now / product
    direction, along = (resid, image)
    for step in range(ITERS):
        answer = answer + alpha * direction
        resid = resid - alpha * along
        if step + 1 < ITERS:
            image = operate(resid, damping)
            norm_next, product = two_products(resid, image)
            ratio = norm_next / norm_now
            alpha = norm_next / (product - ratio * norm_next / alpha)
            direction = resid + ratio * direction
            along = image + ratio * along
            norm_now = norm_next
    return answer


def per_device(init_field, source, damping):
    upper = lax.axis_index("level") == 1
    state = init_field
    older = jnp.where(upper, init_field, jnp.zeros_like(init_field))
    for rounds in range(STEPS + 1):
        if rounds == 0:
            extra = jnp.zeros_like(init_field)
        else:
            incoming = passed_along(state, "level", 1)
            change = incoming - older
            older = incoming
            padded = padded_2(change, (("gx", 0), (YZ, 1)), 1)
            extra = 0.5 * stencil_from(padded, change, damping)
        fresh = solve(state + source + extra, state, damping)
        if rounds == 0:
            state = jnp.where(upper, state, fresh)
        elif rounds == STEPS:
            state = jnp.where(upper, fresh, state)
        else:
            state = fresh
    return state[None]


def solution(mesh):
    split = Mesh(
        mesh.devices.reshape(mesh.shape["level"], mesh.shape["gx"], 8, 4),
        ("level", "gx", "yz_0", "yz_1"),
    )
    placed = (P("gx", YZ, None), P("gx", YZ, None), P("gx", YZ, None))
    return jax.shard_map(
        per_device,
        mesh=split,
        in_specs=placed,
        out_specs=P("level", "gx", YZ, None),
        check_vma=False,
    )
```

profile of v0, /device:TPU:40, one launch (start us, length us, event | category | flops | bytes accessed | tf_op | source)
XLA Modules:
  0.0 816.1 jit_solution(3187403558633558888)
XLA Ops:
  2.0 4.5 collective-permute-start.1
  21.8 6.0 collective-permute-start.6
  34.8 11.1 %all-reduce.111 = (f32[]{:T(128)}, f32[]{:T(128)}) all-reduce(f32[]{:T(128)} %get-tuple-element.28, f32[]{:T(128)} %get-tuple-element.27), channel_id=1, replica_groups=mesh['level'=2,'gx'=4,'yz_0'=8,'yz_1'=4] {'gx'}, use_global_device_ids=true, to_apply=%region_1.2 | all-reduce | flops 2 | bytes 16 | tf_op jit(solution)/shard_map/psum | solution.py:39
  45.9 19.4 %all-reduce.87 = (f32[]{:T(128)}, f32[]{:T(128)}) all-reduce(f32[]{:T(128)} %get-tuple-element.99, f32[]{:T(128)} %get-tuple-element.100), channel_id=1, replica_groups=mesh['level'=2,'gx'=4,'yz_0'=8,'yz_1'=4] {'yz_0'}, use_global_device_ids=true, to_apply=%region_2.3 | all-reduce | flops 2 | bytes 16 | tf_op jit(solution)/shard_map/psum | solution.py:39
  65.3 11.6 %all-reduce.99 = (f32[]{:T(128)}, f32[]{:T(128)}) all-reduce(f32[]{:T(128)} %get-tuple-element.51, f32[]{:T(128)} %get-tuple-element.52), channel_id=1, replica_groups=mesh['level'=2,'gx'=4,'yz_0'=8,'yz_1'=4] {'yz_1'}, use_global_device_ids=true, to_apply=%region_3.4 | all-reduce | flops 2 | bytes 16 | tf_op jit(solution)/shard_map/psum | solution.py:39
  93.4 11.0 %all-reduce.110 = (f32[]{:T(128)}, f32[]{:T(128)}) all-reduce(f32[]{:T(128)} %get-tuple-element.26, f32[]{:T(128)} %get-tuple-element.25), channel_id=1, replica_groups=mesh['level'=2,'gx'=4,'yz_0'=8,'yz_1'=4] {'gx'}, use_global_device_ids=true, to_apply=%region_9.10 | all-reduce | flops 2 | bytes 16 | tf_op jit(solution)/shard_map/psum | solution.py:39
  104.4 16.2 %all-reduce.86 = (f32[]{:T(128)}, f32[]{:T(128)}) all-reduce(f32[]{:T(128)} %get-tuple-element.97, f32[]{:T(128)} %get-tuple-element.98), channel_id=1, replica_groups=mesh['level'=2,'gx'=4,'yz_0'=8,'yz_1'=4] {'yz_0'}, use_global_device_ids=true, to_apply=%region_10.11 | all-reduce | flops 2 | bytes 16 | tf_op jit(solution)/shard_map/psum | solution.py:39
  120.6 12.5 %all-reduce.98 = (f32[]{:T(128)}, f32[]{:T(128)}) all-reduce(f32[]{:T(128)} %get-tuple-element.49, f32[]{:T(128)} %get-tuple-element.50), channel_id=1, replica_groups=mesh['level'=2,'gx'=4,'yz_0'=8,'yz_1'=4] {'yz_1'}, use_global_device_ids=true, to_apply=%region_11.12 | all-reduce | flops 2 | bytes 16 | tf_op jit(solution)/shard_map/psum | solution.py:39
  150.4 11.4 %all-reduce.109 = (f32[]{:T(128)}, f32[]{:T(128)}) all-reduce(f32[]{:T(128)} %get-tuple-element.24, f32[]{:T(128)} %get-tuple-element.23), channel_id=1, replica_groups=mesh['level'=2,'gx'=4,'yz_0'=8,'yz_1'=4] {'gx'}, use_global_device_ids=true, to_apply=%region_17.18 | all-reduce | flops 2 | bytes 16 | tf_op jit(solution)/shard_map/psum | solution.py:39
  161.7 17.3 %all-reduce.85 = (f32[]{:T(128)}, f32[]{:T(128)}) all-reduce(f32[]{:T(128)} %get-tuple-element.95, f32[]{:T(128)} %get-tuple-element.96), channel_id=1, replica_groups=mesh['level'=2,'gx'=4,'yz_0'=8,'yz_1'=4] {'yz_0'}, use_global_device_ids=true, to_apply=%region_18.19 | all-reduce | flops 2 | bytes 16 | tf_op jit(solution)/shard_map/psum | solution.py:39
  179.1 12.5 %all-reduce.97 = (f32[]{:T(128)}, f32[]{:T(128)}) all-reduce(f32[]{:T(128)} %get-tuple-element.47, f32[]{:T(128)} %get-tuple-element.48), channel_id=1, replica_groups=mesh['level'=2,'gx'=4,'yz_0'=8,'yz_1'=4] {'yz_1'}, use_global_device_ids=true, to_apply=%region_19.20 | all-reduce | flops 2 | bytes 16 | tf_op jit(solution)/shard_map/psum | solution.py:39
  207.7 4.5 collective-permute-start.18
  223.9 4.5 collective-permute-start.26
  229.8 6.0 collective-permute-start.27
  242.7 11.0 %all-reduce.108 = (f32[]{:T(128)}, f32[]{:T(128)}) all-reduce(f32[]{:T(128)} %get-tuple-element.22, f32[]{:T(128)} %get-tuple-element.21), channel_id=1, replica_groups=mesh['level'=2,'gx'=4,'yz_0'=8,'yz_1'=4] {'gx'}, use_global_device_ids=true, to_apply=%region_25.26 | all-reduce | flops 2 | bytes 16 | tf_op jit(solution)/shard_map/psum | solution.py:39
  253.7 19.2 %all-reduce.84 = (f32[]{:T(128)}, f32[]{:T(128)}) all-reduce(f32[]{:T(128)} %get-tuple-element.93, f32[]{:T(128)} %get-tuple-element.94), channel_id=1, replica_groups=mesh['level'=2,'gx'=4,'yz_0'=8,'yz_1'=4] {'yz_0'}, use_global_device_ids=true, to_apply=%region_26.27 | all-reduce | flops 2 | bytes 16 | tf_op jit(solution)/shard_map/psum | solution.py:39
  272.9 11.7 %all-reduce.96 = (f32[]{:T(128)}, f32[]{:T(128)}) all-reduce(f32[]{:T(128)} %get-tuple-element.45, f32[]{:T(128)} %get-tuple-element.46), channel_id=1, replica_groups=mesh['level'=2,'gx'=4,'yz_0'=8,'yz_1'=4] {'yz_1'}, use_global_device_ids=true, to_apply=%region_27.28 | all-reduce | flops 2 | bytes 16 | tf_op jit(solution)/shard_map/psum | solution.py:39
  298.7 11.0 %all-reduce.107 = (f32[]{:T(128)}, f32[]{:T(128)}) all-reduce(f32[]{:T(128)} %get-tuple-element.20, f32[]{:T(128)} %get-tuple-element.19), channel_id=1, replica_groups=mesh['level'=2,'gx'=4,'yz_0'=8,'yz_1'=4] {'gx'}, use_global_device_ids=true, to_apply=%region_33.34 | all-reduce | flops 2 | bytes 16 | tf_op jit(solution)/shard_map/psum | solution.py:39
  309.7 17.5 %all-reduce.83 = (f32[]{:T(128)}, f32[]{:T(128)}) all-reduce(f32[]{:T(128)} %get-tuple-element.91, f32[]{:T(128)} %get-tuple-element.92), channel_id=1, replica_groups=mesh['level'=2,'gx'=4,'yz_0'=8,'yz_1'=4] {'yz_0'}, use_global_device_ids=true, to_apply=%region_34.35 | all-reduce | flops 2 | bytes 16 | tf_op jit(solution)/shard_map/psum | solution.py:39
  327.2 12.5 %all-reduce.95 = (f32[]{:T(128)}, f32[]{:T(128)}) all-reduce(f32[]{:T(128)} %get-tuple-element.43, f32[]{:T(128)} %get-tuple-element.44), channel_id=1, replica_groups=mesh['level'=2,'gx'=4,'yz_0'=8,'yz_1'=4] {'yz_1'}, use_global_device_ids=true, to_apply=%region_35.36 | all-reduce | flops 2 | bytes 16 | tf_op jit(solution)/shard_map/psum | solution.py:39
  357.6 11.0 %all-reduce.106 = (f32[]{:T(128)}, f32[]{:T(128)}) all-reduce(f32[]{:T(128)} %get-tuple-element.18, f32[]{:T(128)} %get-tuple-element.17), channel_id=1, replica_groups=mesh['level'=2,'gx'=4,'yz_0'=8,'yz_1'=4] {'gx'}, use_global_device_ids=true, to_apply=%region_41.42 | all-reduce | flops 2 | bytes 16 | tf_op jit(solution)/shard_map/psum | solution.py:39
  368.5 17.5 %all-reduce.82 = (f32[]{:T(128)}, f32[]{:T(128)}) all-reduce(f32[]{:T(128)} %get-tuple-element.89, f32[]{:T(128)} %get-tuple-element.90), channel_id=1, replica_groups=mesh['level'=2,'gx'=4,'yz_0'=8,'yz_1'=4] {'yz_0'}, use_global_device_ids=true, to_apply=%region_42.43 | all-reduce | flops 2 | bytes 16 | tf_op jit(solution)/shard_map/psum | solution.py:39
  386.0 12.6 %all-reduce.94 = (f32[]{:T(128)}, f32[]{:T(128)}) all-reduce(f32[]{:T(128)} %get-tuple-element.41, f32[]{:T(128)} %get-tuple-element.42), channel_id=1, replica_groups=mesh['level'=2,'gx'=4,'yz_0'=8,'yz_1'=4] {'yz_1'}, use_global_device_ids=true, to_apply=%region_43.44 | all-reduce | flops 2 | bytes 16 | tf_op jit(solution)/shard_map/psum | solution.py:39
  413.9 4.5 collective-permute-start.39
  430.1 4.5 collective-permute-start.47
  435.9 6.0 collective-permute-start.48
  448.9 11.0 %all-reduce.105 = (f32[]{:T(128)}, f32[]{:T(128)}) all-reduce(f32[]{:T(128)} %get-tuple-element.16, f32[]{:T(128)} %get-tuple-element.15), channel_id=1, replica_groups=mesh['level'=2,'gx'=4,'yz_0'=8,'yz_1'=4] {'gx'}, use_global_device_ids=true, to_apply=%region_49.50 | all-reduce | flops 2 | bytes 16 | tf_op jit(solution)/shard_map/psum | solution.py:39
  459.9 19.2 %all-reduce.81 = (f32[]{:T(128)}, f32[]{:T(128)}) all-reduce(f32[]{:T(128)} %get-tuple-element.87, f32[]{:T(128)} %get-tuple-element.88), channel_id=1, replica_groups=mesh['level'=2,'gx'=4,'yz_0'=8,'yz_1'=4] {'yz_0'}, use_global_device_ids=true, to_apply=%region_50.51 | all-reduce | flops 2 | bytes 16 | tf_op jit(solution)/shard_map/psum | solution.py:39
  479.1 11.7 %all-reduce.93 = (f32[]{:T(128)}, f32[]{:T(128)}) all-reduce(f32[]{:T(128)} %get-tuple-element.39, f32[]{:T(128)} %get-tuple-element.40), channel_id=1, replica_groups=mesh['level'=2,'gx'=4,'yz_0'=8,'yz_1'=4] {'yz_1'}, use_global_device_ids=true, to_apply=%region_51.52 | all-reduce | flops 2 | bytes 16 | tf_op jit(solution)/shard_map/psum | solution.py:39
  505.5 11.0 %all-reduce.104 = (f32[]{:T(128)}, f32[]{:T(128)}) all-reduce(f32[]{:T(128)} %get-tuple-element.14, f32[]{:T(128)} %get-tuple-element.13), channel_id=1, replica_groups=mesh['level'=2,'gx'=4,'yz_0'=8,'yz_1'=4] {'gx'}, use_global_device_ids=true, to_apply=%region_57.58 | all-reduce | flops 2 | bytes 16 | tf_op jit(solution)/shard_map/psum | solution.py:39
  516.5 17.5 %all-reduce.80 = (f32[]{:T(128)}, f32[]{:T(128)}) all-reduce(f32[]{:T(128)} %get-tuple-element.85, f32[]{:T(128)} %get-tuple-element.86), channel_id=1, replica_groups=mesh['level'=2,'gx'=4,'yz_0'=8,'yz_1'=4] {'yz_0'}, use_global_device_ids=true, to_apply=%region_58.59 | all-reduce | flops 2 | bytes 16 | tf_op jit(solution)/shard_map/psum | solution.py:39
  534.0 12.5 %all-reduce.92 = (f32[]{:T(128)}, f32[]{:T(128)}) all-reduce(f32[]{:T(128)} %get-tuple-element.37, f32[]{:T(128)} %get-tuple-element.38), channel_id=1, replica_groups=mesh['level'=2,'gx'=4,'yz_0'=8,'yz_1'=4] {'yz_1'}, use_global_device_ids=true, to_apply=%region_59.60 | all-reduce | flops 2 | bytes 16 | tf_op jit(solution)/shard_map/psum | solution.py:39
  563.7 11.0 %all-reduce.103 = (f32[]{:T(128)}, f32[]{:T(128)}) all-reduce(f32[]{:T(128)} %get-tuple-element.12, f32[]{:T(128)} %get-tuple-element.11), channel_id=1, replica_groups=mesh['level'=2,'gx'=4,'yz_0'=8,'yz_1'=4] {'gx'}, use_global_device_ids=true, to_apply=%region_65.66 | all-reduce | flops 2 | bytes 16 | tf_op jit(solution)/shard_map/psum | solution.py:39
  574.7 17.5 %all-reduce.79 = (f32[]{:T(128)}, f32[]{:T(128)}) all-reduce(f32[]{:T(128)} %get-tuple-element.83, f32[]{:T(128)} %get-tuple-element.84), channel_id=1, replica_groups=mesh['level'=2,'gx'=4,'yz_0'=8,'yz_1'=4] {'yz_0'}, use_global_device_ids=true, to_apply=%region_66.67 | all-reduce | flops 2 | bytes 16 | tf_op jit(solution)/shard_map/psum | solution.py:39
  592.2 12.5 %all-reduce.91 = (f32[]{:T(128)}, f32[]{:T(128)}) all-reduce(f32[]{:T(128)} %get-tuple-element.35, f32[]{:T(128)} %get-tuple-element.36), channel_id=1, replica_groups=mesh['level'=2,'gx'=4,'yz_0'=8,'yz_1'=4] {'yz_1'}, use_global_device_ids=true, to_apply=%region_67.68 | all-reduce | flops 2 | bytes 16 | tf_op jit(solution)/shard_map/psum | solution.py:39
  615.4 4.0 collective-permute-start.66
  619.9 4.5 collective-permute-start.60
  636.0 4.5 collective-permute-start.68
  641.9 6.0 collective-permute-start.69
  654.9 11.0 %all-reduce.102 = (f32[]{:T(128)}, f32[]{:T(128)}) all-reduce(f32[]{:T(128)} %get-tuple-element.10, f32[]{:T(128)} %get-tuple-element.9), channel_id=1, replica_groups=mesh['level'=2,'gx'=4,'yz_0'=8,'yz_1'=4] {'gx'}, use_global_device_ids=true, to_apply=%region_73.74 | all-reduce | flops 2 | bytes 16 | tf_op jit(solution)/shard_map/psum | solution.py:39
  665.9 19.2 %all-reduce.78 = (f32[]{:T(128)}, f32[]{:T(128)}) all-reduce(f32[]{:T(128)} %get-tuple-element.81, f32[]{:T(128)} %get-tuple-element.82), channel_id=1, replica_groups=mesh['level'=2,'gx'=4,'yz_0'=8,'yz_1'=4] {'yz_0'}, use_global_device_ids=true, to_apply=%region_74.75 | all-reduce | flops 2 | bytes 16 | tf_op jit(solution)/shard_map/psum | solution.py:39
  685.1 11.7 %all-reduce.90 = (f32[]{:T(128)}, f32[]{:T(128)}) all-reduce(f32[]{:T(128)} %get-tuple-element.33, f32[]{:T(128)} %get-tuple-element.34), channel_id=1, replica_groups=mesh['level'=2,'gx'=4,'yz_0'=8,'yz_1'=4] {'yz_1'}, use_global_device_ids=true, to_apply=%region_75.76 | all-reduce | flops 2 | bytes 16 | tf_op jit(solution)/shard_map/psum | solution.py:39
  710.9 11.0 %all-reduce.101 = (f32[]{:T(128)}, f32[]{:T(128)}) all-reduce(f32[]{:T(128)} %get-tuple-element.8, f32[]{:T(128)} %get-tuple-element.7), channel_id=1, replica_groups=mesh['level'=2,'gx'=4,'yz_0'=8,'yz_1'=4] {'gx'}, use_global_device_ids=true, to_apply=%region_81.82 | all-reduce | flops 2 | bytes 16 | tf_op jit(solution)/shard_map/psum | solution.py:39
  721.9 17.5 %all-reduce.77 = (f32[]{:T(128)}, f32[]{:T(128)}) all-reduce(f32[]{:T(128)} %get-tuple-element.79, f32[]{:T(128)} %get-tuple-element.80), channel_id=1, replica_groups=mesh['level'=2,'gx'=4,'yz_0'=8,'yz_1'=4] {'yz_0'}, use_global_device_ids=true, to_apply=%region_82.83 | all-reduce | flops 2 | bytes 16 | tf_op jit(solution)/shard_map/psum | solution.py:39
  739.5 12.5 %all-reduce.89 = (f32[]{:T(128)}, f32[]{:T(128)}) all-reduce(f32[]{:T(128)} %get-tuple-element.31, f32[]{:T(128)} %get-tuple-element.32), channel_id=1, replica_groups=mesh['level'=2,'gx'=4,'yz_0'=8,'yz_1'=4] {'yz_1'}, use_global_device_ids=true, to_apply=%region_83.84 | all-reduce | flops 2 | bytes 16 | tf_op jit(solution)/shard_map/psum | solution.py:39
  770.1 11.0 %all-reduce.100 = (f32[]{:T(128)}, f32[]{:T(128)}) all-reduce(f32[]{:T(128)} %get-tuple-element.6, f32[]{:T(128)} %get-tuple-element.5), channel_id=1, replica_groups=mesh['level'=2,'gx'=4,'yz_0'=8,'yz_1'=4] {'gx'}, use_global_device_ids=true, to_apply=%region_89.90 | all-reduce | flops 2 | bytes 16 | tf_op jit(solution)/shard_map/psum | solution.py:39
  781.2 17.5 %all-reduce.76 = (f32[]{:T(128)}, f32[]{:T(128)}) all-reduce(f32[]{:T(128)} %get-tuple-element.77, f32[]{:T(128)} %get-tuple-element.78), channel_id=1, replica_groups=mesh['level'=2,'gx'=4,'yz_0'=8,'yz_1'=4] {'yz_0'}, use_global_device_ids=true, to_apply=%region_90.91 | all-reduce | flops 2 | bytes 16 | tf_op jit(solution)/shard_map/psum | solution.py:39
  798.6 12.5 %all-reduce.88 = (f32[]{:T(128)}, f32[]{:T(128)}) all-reduce(f32[]{:T(128)} %get-tuple-element.29, f32[]{:T(128)} %get-tuple-element.30), channel_id=1, replica_groups=mesh['level'=2,'gx'=4,'yz_0'=8,'yz_1'=4] {'yz_1'}, use_global_device_ids=true, to_apply=%region_91.92 | all-reduce | flops 2 | bytes 16 | tf_op jit(solution)/shard_map/psum | solution.py:39
  (257 shorter events, 222.7 us)
Async XLA Ops:
  0.7 14.4 %collective-permute-start = (f32[1,16,256]{2,1,0:T(8,128)S(1)}, f32[1,16,256]{2,1,0:T(8,128)S(1)}, u32[]{:S(2)}, u32[]{:S(2)}) collective-permute-start(f32[1,16,256]{2,1,0:T(8,128)S(1)} %get-tuple-element.221), channel_id=1, source_target_pairs={{32,0},{64,32},{96,64},{33,1},{65,33},{97,65},{34,2},{66,34},{98,6... | collective-permute-start | bytes 49160 | tf_op jit(solution)/shard_map/ppermute | solution.py:27
  2.0 13.1 %collective-permute-start.1 = (f32[1,16,256]{2,1,0:T(8,128)S(1)}, f32[1,16,256]{2,1,0:T(8,128)S(1)}, u32[]{:S(2)}, u32[]{:S(2)}) collective-permute-start(f32[1,16,256]{2,1,0:T(8,128)S(1)} %get-tuple-element.222), channel_id=1, source_target_pairs={{0,32},{32,64},{64,96},{1,33},{33,65},{65,97},{2,34},{34,66},{66,9... | collective-permute-start | bytes 49160 | tf_op jit(solution)/shard_map/ppermute | solution.py:26
  7.7 7.5 collective-permute-start.2
  17.1 12.9 %collective-permute-start.5 = (f32[1,16,256]{2,1,0:T(8,128)S(1)}, f32[1,16,256]{2,1,0:T(8,128)S(1)}, u32[]{:S(2)}, u32[]{:S(2)}) collective-permute-start(f32[1,16,256]{2,1,0:T(8,128)S(1)} %get-tuple-element.213), channel_id=1, source_target_pairs={{0,32},{32,64},{64,96},{1,33},{33,65},{65,97},{2,34},{34,66},{66,9... | collective-permute-start | bytes 49160 | tf_op jit(solution)/shard_map/ppermute | solution.py:26
  20.5 9.5 %collective-permute-start.4 = (f32[1,16,256]{2,1,0:T(8,128)S(1)}, f32[1,16,256]{2,1,0:T(8,128)S(1)}, u32[]{:S(2)}, u32[]{:S(2)}) collective-permute-start(f32[1,16,256]{2,1,0:T(8,128)S(1)} %get-tuple-element.214), channel_id=1, source_target_pairs={{32,0},{64,32},{96,64},{33,1},{65,33},{97,65},{34,2},{66,34},{98,6... | collective-permute-start | bytes 49160 | tf_op jit(solution)/shard_map/ppermute | solution.py:27
  21.8 8.2 %collective-permute-start.6 = (f32[32,1,256]{2,1,0:T(1,128)S(1)}, f32[32,1,256]{2,1,0:T(1,128)S(1)}, u32[]{:S(2)}, u32[]{:S(2)}) collective-permute-start(f32[32,1,256]{2,1,0:T(1,128)S(1)} %get-tuple-element.211), channel_id=1, source_target_pairs={{1,0},{2,1},{3,2},{4,3},{5,4},{6,5},{7,6},{8,7},{9,8},{10,9},{11,1... | collective-permute-start | bytes 98312 | tf_op jit(solution)/shard_map/ppermute | solution.py:27
  78.4 10.1 %collective-permute-start.9 = (f32[1,16,256]{2,1,0:T(8,128)S(1)}, f32[1,16,256]{2,1,0:T(8,128)S(1)}, u32[]{:S(2)}, u32[]{:S(2)}) collective-permute-start(f32[1,16,256]{2,1,0:T(8,128)S(1)} %get-tuple-element.207), channel_id=1, source_target_pairs={{0,32},{32,64},{64,96},{1,33},{33,65},{65,97},{2,34},{34,66},{66,9... | collective-permute-start | bytes 49160 | tf_op jit(solution)/shard_map/ppermute | solution.py:26
  138.8 8.7 %collective-permute-start.13 = (f32[1,16,256]{2,1,0:T(8,128)S(1)}, f32[1,16,256]{2,1,0:T(8,128)S(1)}, u32[]{:S(2)}, u32[]{:S(2)}) collective-permute-start(f32[1,16,256]{2,1,0:T(8,128)S(1)} %get-tuple-element.203), channel_id=1, source_target_pairs={{0,32},{32,64},{64,96},{1,33},{33,65},{65,97},{2,34},{34,66},{66,9... | collective-permute-start | bytes 49160 | tf_op jit(solution)/shard_map/ppermute | solution.py:26
  140.1 7.4 collective-permute-start.12
  195.7 11.1 %collective-permute-start.16 = (f32[32,16,256]{2,1,0:T(8,128)S(1)}, f32[32,16,256]{2,1,0:T(8,128)S(1)}, u32[]{:S(2)}, u32[]{:S(2)}) collective-permute-start(f32[32,16,256]{2,1,0:T(8,128)S(1)} %add_select_fusion), channel_id=1, source_target_pairs={{0,128},{1,129},{2,130},{3,131},{4,132},{5,133},{6,134},{7,135},{8... | collective-permute-start | bytes 1572872 | tf_op jit(solution)/shard_map/ppermute | solution.py:45
  197.1 15.2 %collective-permute-start.22 = (f32[1,16,256]{2,1,0:T(8,128)S(1)}, f32[1,16,256]{2,1,0:T(8,128)S(1)}, u32[]{:S(2)}, u32[]{:S(2)}) collective-permute-start(f32[1,16,256]{2,1,0:T(8,128)S(1)} %get-tuple-element.197), channel_id=1, source_target_pairs={{0,32},{32,64},{64,96},{1,33},{33,65},{65,97},{2,34},{34,66},{66,9... | collective-permute-start | bytes 49160 | tf_op jit(solution)/shard_map/ppermute | solution.py:26
  199.4 14.2 %collective-permute-start.21 = (f32[1,16,256]{2,1,0:T(8,128)S(1)}, f32[1,16,256]{2,1,0:T(8,128)S(1)}, u32[]{:S(2)}, u32[]{:S(2)}) collective-permute-start(f32[1,16,256]{2,1,0:T(8,128)S(1)} %get-tuple-element.198), channel_id=1, source_target_pairs={{32,0},{64,32},{96,64},{33,1},{65,33},{97,65},{34,2},{66,34},{98,6... | collective-permute-start | bytes 49160 | tf_op jit(solution)/shard_map/ppermute | solution.py:27
  200.8 14.7 %collective-permute-start.23 = (f32[32,1,256]{2,1,0:T(1,128)S(1)}, f32[32,1,256]{2,1,0:T(1,128)S(1)}, u32[]{:S(2)}, u32[]{:S(2)}) collective-permute-start(f32[32,1,256]{2,1,0:T(1,128)S(1)} %get-tuple-element.195), channel_id=1, source_target_pairs={{1,0},{2,1},{3,2},{4,3},{5,4},{6,5},{7,6},{8,7},{9,8},{10,9},{11,1... | collective-permute-start | bytes 98312 | tf_op jit(solution)/shard_map/ppermute | solution.py:27
  202.7 17.1 %collective-permute-start.24 = (f32[32,1,256]{2,1,0:T(1,128)S(1)}, f32[32,1,256]{2,1,0:T(1,128)S(1)}, u32[]{:S(2)}, u32[]{:S(2)}) collective-permute-start(f32[32,1,256]{2,1,0:T(1,128)S(1)} %get-tuple-element.196), channel_id=1, source_target_pairs={{0,1},{1,2},{2,3},{3,4},{4,5},{5,6},{6,7},{7,8},{8,9},{9,10},{10,1... | collective-permute-start | bytes 98312 | tf_op jit(solution)/shard_map/ppermute | solution.py:26
  207.7 12.1 %collective-permute-start.18 = (f32[1,16,256]{2,1,0:T(8,128)S(1)}, f32[1,16,256]{2,1,0:T(8,128)S(1)}, u32[]{:S(2)}, u32[]{:S(2)}) collective-permute-start(f32[1,16,256]{2,1,0:T(8,128)S(1)} %get-tuple-element.193), channel_id=1, source_target_pairs={{0,32},{32,64},{64,96},{1,33},{33,65},{65,97},{2,34},{34,66},{66,9... | collective-permute-start | bytes 49160 | tf_op jit(solution)/shard_map/ppermute | solution.py:26
  212.3 7.6 collective-permute-start.17
  215.6 7.5 collective-permute-start.20
  223.9 14.0 %collective-permute-start.26 = (f32[1,16,256]{2,1,0:T(8,128)S(1)}, f32[1,16,256]{2,1,0:T(8,128)S(1)}, u32[]{:S(2)}, u32[]{:S(2)}) collective-permute-start(f32[1,16,256]{2,1,0:T(8,128)S(1)} %get-tuple-element.183), channel_id=1, source_target_pairs={{0,32},{32,64},{64,96},{1,33},{33,65},{65,97},{2,34},{34,66},{66,9... | collective-permute-start | bytes 49160 | tf_op jit(solution)/shard_map/ppermute | solution.py:26
  228.5 9.5 %collective-permute-start.25 = (f32[1,16,256]{2,1,0:T(8,128)S(1)}, f32[1,16,256]{2,1,0:T(8,128)S(1)}, u32[]{:S(2)}, u32[]{:S(2)}) collective-permute-start(f32[1,16,256]{2,1,0:T(8,128)S(1)} %get-tuple-element.184), channel_id=1, source_target_pairs={{32,0},{64,32},{96,64},{33,1},{65,33},{97,65},{34,2},{66,34},{98,6... | collective-permute-start | bytes 49160 | tf_op jit(solution)/shard_map/ppermute | solution.py:27
  229.8 8.2 %collective-permute-start.27 = (f32[32,1,256]{2,1,0:T(1,128)S(1)}, f32[32,1,256]{2,1,0:T(1,128)S(1)}, u32[]{:S(2)}, u32[]{:S(2)}) collective-permute-start(f32[32,1,256]{2,1,0:T(1,128)S(1)} %get-tuple-element.181), channel_id=1, source_target_pairs={{1,0},{2,1},{3,2},{4,3},{5,4},{6,5},{7,6},{8,7},{9,8},{10,9},{11,1... | collective-permute-start | bytes 98312 | tf_op jit(solution)/shard_map/ppermute | solution.py:27
  286.1 9.0 %collective-permute-start.30 = (f32[1,16,256]{2,1,0:T(8,128)S(1)}, f32[1,16,256]{2,1,0:T(8,128)S(1)}, u32[]{:S(2)}, u32[]{:S(2)}) collective-permute-start(f32[1,16,256]{2,1,0:T(8,128)S(1)} %get-tuple-element.177), channel_id=1, source_target_pairs={{0,32},{32,64},{64,96},{1,33},{33,65},{65,97},{2,34},{34,66},{66,9... | collective-permute-start | bytes 49160 | tf_op jit(solution)/shard_map/ppermute | solution.py:26
  345.1 9.7 %collective-permute-start.34 = (f32[1,16,256]{2,1,0:T(8,128)S(1)}, f32[1,16,256]{2,1,0:T(8,128)S(1)}, u32[]{:S(2)}, u32[]{:S(2)}) collective-permute-start(f32[1,16,256]{2,1,0:T(8,128)S(1)} %get-tuple-element.173), channel_id=1, source_target_pairs={{0,32},{32,64},{64,96},{1,33},{33,65},{65,97},{2,34},{34,66},{66,9... | collective-permute-start | bytes 49160 | tf_op jit(solution)/shard_map/ppermute | solution.py:26
  402.4 10.6 %collective-permute-start.37 = (f32[32,16,256]{2,1,0:T(8,128)S(1)}, f32[32,16,256]{2,1,0:T(8,128)S(1)}, u32[]{:S(2)}, u32[]{:S(2)}) collective-permute-start(f32[32,16,256]{2,1,0:T(8,128)S(1)} %multiply_add_fusion.1), channel_id=1, source_target_pairs={{0,128},{1,129},{2,130},{3,131},{4,132},{5,133},{6,134},{7,135},{8... | collective-permute-start | bytes 1572872 | tf_op jit(solution)/shard_map/ppermute | solution.py:45
  403.8 14.7 %collective-permute-start.43 = (f32[1,16,256]{2,1,0:T(8,128)S(1)}, f32[1,16,256]{2,1,0:T(8,128)S(1)}, u32[]{:S(2)}, u32[]{:S(2)}) collective-permute-start(f32[1,16,256]{2,1,0:T(8,128)S(1)} %get-tuple-element.167), channel_id=1, source_target_pairs={{0,32},{32,64},{64,96},{1,33},{33,65},{65,97},{2,34},{34,66},{66,9... | collective-permute-start | bytes 49160 | tf_op jit(solution)/shard_map/ppermute | solution.py:26
  405.4 14.3 %collective-permute-start.42 = (f32[1,16,256]{2,1,0:T(8,128)S(1)}, f32[1,16,256]{2,1,0:T(8,128)S(1)}, u32[]{:S(2)}, u32[]{:S(2)}) collective-permute-start(f32[1,16,256]{2,1,0:T(8,128)S(1)} %get-tuple-element.168), channel_id=1, source_target_pairs={{32,0},{64,32},{96,64},{33,1},{65,33},{97,65},{34,2},{66,34},{98,6... | collective-permute-start | bytes 49160 | tf_op jit(solution)/shard_map/ppermute | solution.py:27
  406.8 14.9 %collective-permute-start.44 = (f32[32,1,256]{2,1,0:T(1,128)S(1)}, f32[32,1,256]{2,1,0:T(1,128)S(1)}, u32[]{:S(2)}, u32[]{:S(2)}) collective-permute-start(f32[32,1,256]{2,1,0:T(1,128)S(1)} %get-tuple-element.165), channel_id=1, source_target_pairs={{1,0},{2,1},{3,2},{4,3},{5,4},{6,5},{7,6},{8,7},{9,8},{10,9},{11,1... | collective-permute-start | bytes 98312 | tf_op jit(solution)/shard_map/ppermute | solution.py:27
  408.7 17.2 %collective-permute-start.45 = (f32[32,1,256]{2,1,0:T(1,128)S(1)}, f32[32,1,256]{2,1,0:T(1,128)S(1)}, u32[]{:S(2)}, u32[]{:S(2)}) collective-permute-start(f32[32,1,256]{2,1,0:T(1,128)S(1)} %get-tuple-element.166), channel_id=1, source_target_pairs={{0,1},{1,2},{2,3},{3,4},{4,5},{5,6},{6,7},{7,8},{8,9},{9,10},{10,1... | collective-permute-start | bytes 98312 | tf_op jit(solution)/shard_map/ppermute | solution.py:26
  413.9 12.1 %collective-permute-start.39 = (f32[1,16,256]{2,1,0:T(8,128)S(1)}, f32[1,16,256]{2,1,0:T(8,128)S(1)}, u32[]{:S(2)}, u32[]{:S(2)}) collective-permute-start(f32[1,16,256]{2,1,0:T(8,128)S(1)} %get-tuple-element.163), channel_id=1, source_target_pairs={{0,32},{32,64},{64,96},{1,33},{33,65},{65,97},{2,34},{34,66},{66,9... | collective-permute-start | bytes 49160 | tf_op jit(solution)/shard_map/ppermute | solution.py:26
  418.4 7.6 collective-permute-start.38
  421.7 7.5 collective-permute-start.41
  430.1 14.0 %collective-permute-start.47 = (f32[1,16,256]{2,1,0:T(8,128)S(1)}, f32[1,16,256]{2,1,0:T(8,128)S(1)}, u32[]{:S(2)}, u32[]{:S(2)}) collective-permute-start(f32[1,16,256]{2,1,0:T(8,128)S(1)} %get-tuple-element.153), channel_id=1, source_target_pairs={{0,32},{32,64},{64,96},{1,33},{33,65},{65,97},{2,34},{34,66},{66,9... | collective-permute-start | bytes 49160 | tf_op jit(solution)/shard_map/ppermute | solution.py:26
  434.6 9.5 %collective-permute-start.46 = (f32[1,16,256]{2,1,0:T(8,128)S(1)}, f32[1,16,256]{2,1,0:T(8,128)S(1)}, u32[]{:S(2)}, u32[]{:S(2)}) collective-permute-start(f32[1,16,256]{2,1,0:T(8,128)S(1)} %get-tuple-element.154), channel_id=1, source_target_pairs={{32,0},{64,32},{96,64},{33,1},{65,33},{97,65},{34,2},{66,34},{98,6... | collective-permute-start | bytes 49160 | tf_op jit(solution)/shard_map/ppermute | solution.py:27
  435.9 8.2 %collective-permute-start.48 = (f32[32,1,256]{2,1,0:T(1,128)S(1)}, f32[32,1,256]{2,1,0:T(1,128)S(1)}, u32[]{:S(2)}, u32[]{:S(2)}) collective-permute-start(f32[32,1,256]{2,1,0:T(1,128)S(1)} %get-tuple-element.151), channel_id=1, source_target_pairs={{1,0},{2,1},{3,2},{4,3},{5,4},{6,5},{7,6},{8,7},{9,8},{10,9},{11,1... | collective-permute-start | bytes 98312 | tf_op jit(solution)/shard_map/ppermute | solution.py:27
  492.2 9.7 %collective-permute-start.51 = (f32[1,16,256]{2,1,0:T(8,128)S(1)}, f32[1,16,256]{2,1,0:T(8,128)S(1)}, u32[]{:S(2)}, u32[]{:S(2)}) collective-permute-start(f32[1,16,256]{2,1,0:T(8,128)S(1)} %get-tuple-element.147), channel_id=1, source_target_pairs={{0,32},{32,64},{64,96},{1,33},{33,65},{65,97},{2,34},{34,66},{66,9... | collective-permute-start | bytes 49160 | tf_op jit(solution)/shard_map/ppermute | solution.py:26
  551.9 9.1 %collective-permute-start.55 = (f32[1,16,256]{2,1,0:T(8,128)S(1)}, f32[1,16,256]{2,1,0:T(8,128)S(1)}, u32[]{:S(2)}, u32[]{:S(2)}) collective-permute-start(f32[1,16,256]{2,1,0:T(8,128)S(1)} %get-tuple-element.143), channel_id=1, source_target_pairs={{0,32},{32,64},{64,96},{1,33},{33,65},{65,97},{2,34},{34,66},{66,9... | collective-permute-start | bytes 49160 | tf_op jit(solution)/shard_map/ppermute | solution.py:26
  608.4 11.3 %collective-permute-start.58 = (f32[32,16,256]{2,1,0:T(8,128)S(1)}, f32[32,16,256]{2,1,0:T(8,128)S(1)}, u32[]{:S(2)}, u32[]{:S(2)}) collective-permute-start(f32[32,16,256]{2,1,0:T(8,128)S(1)} %multiply_add_fusion), channel_id=1, source_target_pairs={{0,128},{1,129},{2,130},{3,131},{4,132},{5,133},{6,134},{7,135},{8... | collective-permute-start | bytes 1572872 | tf_op jit(solution)/shard_map/ppermute | solution.py:45
  609.7 14.7 %collective-permute-start.64 = (f32[1,16,256]{2,1,0:T(8,128)S(1)}, f32[1,16,256]{2,1,0:T(8,128)S(1)}, u32[]{:S(2)}, u32[]{:S(2)}) collective-permute-start(f32[1,16,256]{2,1,0:T(8,128)S(1)} %get-tuple-element.137), channel_id=1, source_target_pairs={{0,32},{32,64},{64,96},{1,33},{33,65},{65,97},{2,34},{34,66},{66,9... | collective-permute-start | bytes 49160 | tf_op jit(solution)/shard_map/ppermute | solution.py:26
  612.1 13.6 %collective-permute-start.63 = (f32[1,16,256]{2,1,0:T(8,128)S(1)}, f32[1,16,256]{2,1,0:T(8,128)S(1)}, u32[]{:S(2)}, u32[]{:S(2)}) collective-permute-start(f32[1,16,256]{2,1,0:T(8,128)S(1)} %get-tuple-element.138), channel_id=1, source_target_pairs={{32,0},{64,32},{96,64},{33,1},{65,33},{97,65},{34,2},{66,34},{98,6... | collective-permute-start | bytes 49160 | tf_op jit(solution)/shard_map/ppermute | solution.py:27
  613.5 14.2 %collective-permute-start.65 = (f32[32,1,256]{2,1,0:T(1,128)S(1)}, f32[32,1,256]{2,1,0:T(1,128)S(1)}, u32[]{:S(2)}, u32[]{:S(2)}) collective-permute-start(f32[32,1,256]{2,1,0:T(1,128)S(1)} %get-tuple-element.135), channel_id=1, source_target_pairs={{1,0},{2,1},{3,2},{4,3},{5,4},{6,5},{7,6},{8,7},{9,8},{10,9},{11,1... | collective-permute-start | bytes 98312 | tf_op jit(solution)/shard_map/ppermute | solution.py:27
  615.4 16.5 %collective-permute-start.66 = (f32[32,1,256]{2,1,0:T(1,128)S(1)}, f32[32,1,256]{2,1,0:T(1,128)S(1)}, u32[]{:S(2)}, u32[]{:S(2)}) collective-permute-start(f32[32,1,256]{2,1,0:T(1,128)S(1)} %get-tuple-element.136), channel_id=1, source_target_pairs={{0,1},{1,2},{2,3},{3,4},{4,5},{5,6},{6,7},{7,8},{8,9},{9,10},{10,1... | collective-permute-start | bytes 98312 | tf_op jit(solution)/shard_map/ppermute | solution.py:26
  619.9 12.1 %collective-permute-start.60 = (f32[1,16,256]{2,1,0:T(8,128)S(1)}, f32[1,16,256]{2,1,0:T(8,128)S(1)}, u32[]{:S(2)}, u32[]{:S(2)}) collective-permute-start(f32[1,16,256]{2,1,0:T(8,128)S(1)} %get-tuple-element.133), channel_id=1, source_target_pairs={{0,32},{32,64},{64,96},{1,33},{33,65},{65,97},{2,34},{34,66},{66,9... | collective-permute-start | bytes 49160 | tf_op jit(solution)/shard_map/ppermute | solution.py:26
  624.4 7.6 collective-permute-start.59
  627.7 7.5 collective-permute-start.62
  636.0 14.0 %collective-permute-start.68 = (f32[1,16,256]{2,1,0:T(8,128)S(1)}, f32[1,16,256]{2,1,0:T(8,128)S(1)}, u32[]{:S(2)}, u32[]{:S(2)}) collective-permute-start(f32[1,16,256]{2,1,0:T(8,128)S(1)} %get-tuple-element.123), channel_id=1, source_target_pairs={{0,32},{32,64},{64,96},{1,33},{33,65},{65,97},{2,34},{34,66},{66,9... | collective-permute-start | bytes 49160 | tf_op jit(solution)/shard_map/ppermute | solution.py:26
  640.6 9.5 %collective-permute-start.67 = (f32[1,16,256]{2,1,0:T(8,128)S(1)}, f32[1,16,256]{2,1,0:T(8,128)S(1)}, u32[]{:S(2)}, u32[]{:S(2)}) collective-permute-start(f32[1,16,256]{2,1,0:T(8,128)S(1)} %get-tuple-element.124), channel_id=1, source_target_pairs={{32,0},{64,32},{96,64},{33,1},{65,33},{97,65},{34,2},{66,34},{98,6... | collective-permute-start | bytes 49160 | tf_op jit(solution)/shard_map/ppermute | solution.py:27
  641.9 8.2 %collective-permute-start.69 = (f32[32,1,256]{2,1,0:T(1,128)S(1)}, f32[32,1,256]{2,1,0:T(1,128)S(1)}, u32[]{:S(2)}, u32[]{:S(2)}) collective-permute-start(f32[32,1,256]{2,1,0:T(1,128)S(1)} %get-tuple-element.121), channel_id=1, source_target_pairs={{1,0},{2,1},{3,2},{4,3},{5,4},{6,5},{7,6},{8,7},{9,8},{10,9},{11,1... | collective-permute-start | bytes 98312 | tf_op jit(solution)/shard_map/ppermute | solution.py:27
  698.3 9.0 %collective-permute-start.72 = (f32[1,16,256]{2,1,0:T(8,128)S(1)}, f32[1,16,256]{2,1,0:T(8,128)S(1)}, u32[]{:S(2)}, u32[]{:S(2)}) collective-permute-start(f32[1,16,256]{2,1,0:T(8,128)S(1)} %get-tuple-element.117), channel_id=1, source_target_pairs={{0,32},{32,64},{64,96},{1,33},{33,65},{65,97},{2,34},{34,66},{66,9... | collective-permute-start | bytes 49160 | tf_op jit(solution)/shard_map/ppermute | solution.py:26
  757.6 9.7 %collective-permute-start.76 = (f32[1,16,256]{2,1,0:T(8,128)S(1)}, f32[1,16,256]{2,1,0:T(8,128)S(1)}, u32[]{:S(2)}, u32[]{:S(2)}) collective-permute-start(f32[1,16,256]{2,1,0:T(8,128)S(1)} %get-tuple-element.113), channel_id=1, source_target_pairs={{0,32},{32,64},{64,96},{1,33},{33,65},{65,97},{2,34},{34,66},{66,9... | collective-permute-start | bytes 49160 | tf_op jit(solution)/shard_map/ppermute | solution.py:26
  (41 other events, 237.5 us)
where the time goes:
time: 820 us; the launch traced here: 816 us
  blocking collectives  495 us (60%)
  starting transfers between devices  206 us (25%)
  waiting for transfers between devices  40.2 us (5%)
  between operations  38.5 us (5%)
  other arithmetic  26.8 us (3%)
  local copies, waits for them, and re-layouts  9.39 us (1%)
    psum x36, blocking collectives, one_axis_at_a_time(): return functools.reduce(lax.psum, axes, shard)  495 us
    ppermute x38, starting transfers between devices, padded_2(): lax.ppermute(last, axis, up)  124 us
    ppermute x38, starting transfers between devices, padded_2(): lax.ppermute(initial, axis, [(b, a) for a, b in up])  78 us
    ppermute x38, waiting for transfers between devices, padded_2(): lax.ppermute(last, axis, up)  40.1 us
    reduce_sum x12, other arithmetic, two_products(): jnp.sum(resid * image)  16.6 us
  transfers between devices with their start and end apart: 79, of which 16 were waited for; matrix products, arithmetic and copies ran while one was open for 1% of the time, Pallas kernels for 0%

commit v1 on v0

v1 whole, which is shorter than its diff:
```python
import functools

import jax
import jax.numpy as jnp
import numpy as np
from jax import lax
from jax.experimental import pallas as pl
from jax.experimental.pallas import tpu as pltpu
from jax.sharding import PartitionSpec as P

STEPS = 3
ITERS = 3
MESH = pl.DeviceIdType.MESH
F32 = jnp.float32

LOW, HIGH = 1.05, 15.0
MID, HALF = (LOW + HIGH) / 2, (HIGH - LOW) / 2
W = 4


def block_polynomial():
    cheb = np.polynomial.chebyshev
    low, high = 2.0, 13.5

    def third(lam):
        x = (lam - (low + high) / 2) / ((high - low) / 2)
        return 4 * x**3 - 3 * x

    nodes = np.cos(np.pi * (np.arange(4) + 0.5) / 4)
    lam = MID + HALF * nodes
    rho = cheb.chebfit(nodes, (1 + (lam - 1) * third(lam) / third(0.0)) / lam, 3)
    return [float(c) for c in cheb.chebmul(rho, [0.0, 1.0])]


PSI = block_polynomial()


def zsum(v0, v1, first, last):
    a0, a1 = pltpu.roll(v0, 1, 1), pltpu.roll(v1, 1, 1)
    b0, b1 = pltpu.roll(v0, 127, 1), pltpu.roll(v1, 127, 1)
    n0 = jnp.where(first, 0.0, a0) + jnp.where(last, b1, b0)
    n1 = jnp.where(first, a0, a1) + jnp.where(last, 0.0, b1)
    return n0, n1


def recurrences(nu):
    c0, c1, c2, c3, c4 = PSI

    def pattern(rows, values):
        j = lax.rem(lax.broadcasted_iota(jnp.int32, (rows, 128), 0), 4)
        out = jnp.full((rows, 128), values[3], F32)
        for q in range(3):
            out = jnp.where(j == q, values[q], out)
        return out

    bands = {
        1: (1.0, 0.5, 0.5, 0.5 / c4),
        -1: (0.0, 0.5, 0.5, 0.5 - 0.5 * c2 / c4),
        0: (0.0, 0.0, 0.0, -0.5 * c3 / c4),
        -2: (0.0, 0.0, 0.0, -0.5 * c1 / c4),
        -3: (0.0, 0.0, 0.0, -0.5 * c0 / c4),
    }
    long = {o: pattern(24, v) for o, v in bands.items()}
    short = {o: pattern(16, v) for o, v in bands.items()}

    def shifted(v, o):
        rows = v.shape[0]
        return v if o % rows == 0 else pltpu.roll(v, o % rows, 0)

    def times(z, shift):
        f, m = z
        fx = sum(shifted(f * short[o], o) for o in bands)
        mx = sum(long[o] * shifted(m, -o) for o in bands)
        return fx + shift * f, mx + shift * m

    def inner(y, z):
        return jnp.sum(y[0] * z[1][:16], axis=0, keepdims=True)

    def axpy(y, s, z):
        return y[0] + s * z[0], y[1] + s * z[1]

    one = jnp.where(lax.broadcasted_iota(jnp.int32, (16, 128), 0) == 0, 1.0, 0.0).astype(F32)
    start = (one, nu)

    def solve(resid, answer):
        direction = resid
        norm = inner(resid, resid)
        for step in range(ITERS):
            image = times(direction, MID / HALF)
            alpha = norm / inner(direction, image)
            answer = axpy(answer, alpha, direction) if answer else (alpha * direction[0], alpha * direction[1])
            if step + 1 < ITERS:
                resid = axpy(resid, -alpha, image)
                following = inner(resid, resid)
                direction = axpy(resid, following / norm, direction)
                norm = following
        return answer

    back = (MID - 1.0) / HALF
    states = [None]
    corrected = None
    for step in range(STEPS):
        state = states[-1]
        resid = axpy(start, -1.0, times(state, back)) if state else start
        states.append(solve(resid, state))
        change = axpy(states[-1], -1.0, state) if state else states[-1]
        inside = axpy(corrected, -0.5, change) if corrected else (-0.5 * change[0], -0.5 * change[1])
        resid = axpy(start, -1.0, times(inside, back))
        corrected = solve(resid, corrected)
    return states[-1][0] * (1.0 / HALF), corrected[0] * (1.0 / HALF)


def kernel(
    init_hbm, source_hbm, damping_hbm, out_hbm,
    vec, diag, init, source, damping, ys, yr, ps, pr, sums, part_a, part_b, mine, theirs,
    local_sem, init_send, init_recv, ghost_send, ghost_recv,
    a_send, a_recv, b_send, b_recv, out_sem, out_send, out_recv,
):
    c = lax.axis_index("level")
    gx = lax.axis_index("gx")
    yz = lax.axis_index("yz")
    other = 1 - c
    beyond = lax.rem(gx + 2 * c + 3, 4)
    above, below = lax.rem(yz + 1, 32), lax.rem(yz + 31, 32)
    far, near = (other, beyond, yz), (other, gx, yz)
    up, down = (c, gx, above), (c, gx, below)
    far_up, far_down = (other, beyond, above), (other, beyond, below)
    near_up, near_down = (other, gx, above), (other, gx, below)
    neighbours = (far, near, up, down, far_up, far_down, near_up, near_down)
    y, z = lax.rem(yz, 4), lax.div(yz, 4)
    plane_slot = gx * 8 + c * 4 + y

    def plane_mate(k):
        slot = lax.rem(plane_slot + k, 32)
        return slot, (lax.rem(lax.div(slot, 4), 2), lax.div(slot, 8), z * 4 + lax.rem(slot, 4))

    def line_mate(k):
        slot = lax.rem(z + k, 8)
        return slot, (c, gx, slot * 4 + y)

    barrier = pltpu.get_barrier_semaphore()
    for device in neighbours:
        pl.semaphore_signal(barrier, inc=1, device_id=device, device_id_type=MESH)

    own = pl.ds(c * 16, 16)
    loads = [
        pltpu.make_async_copy(damping_hbm.at[own], damping, local_sem.at[0]),
        pltpu.make_async_copy(init_hbm.at[own], init.at[pl.ds(1, 16)], local_sem.at[1]),
        pltpu.make_async_copy(
            init_hbm.at[pl.ds(16 - c, 1)], init.at[pl.ds(17 - 17 * c, 1)], local_sem.at[2]
        ),
        pltpu.make_async_copy(source_hbm.at[own], source, local_sem.at[3]),
    ]
    for load in loads:
        load.start()

    def greet_plane(k, carry):
        pl.semaphore_signal(barrier, inc=1, device_id=plane_mate(k)[1], device_id_type=MESH)
        return carry

    lax.fori_loop(1, 32, greet_plane, 0)
    for k in range(1, 8):
        pl.semaphore_signal(barrier, inc=1, device_id=line_mate(k)[1], device_id_type=MESH)

    lane = lax.broadcasted_iota(jnp.int32, (24, 128), 1)
    first, last = lane == 0, lane == 127
    row = lax.broadcasted_iota(jnp.int32, (16, 128), 0)
    top, bottom = row == 0, row == 15
    has_low = jnp.where(yz > 0, 1.0, 0.0).astype(F32)
    has_high = jnp.where(yz < 31, 1.0, 0.0).astype(F32)
    x_low = jnp.where(gx + c > 0, 1.0, 0.0).astype(F32)
    x_high = jnp.where(gx + c < 4, 1.0, 0.0).astype(F32)
    ghost_row = lax.broadcasted_iota(jnp.int32, (8, 128), 0)
    inside = jnp.where(ghost_row < 4, has_high, has_low)

    def send(src, dst, sends, recvs, device):
        copy = pltpu.make_async_remote_copy(
            src_ref=src, dst_ref=dst, send_sem=sends, recv_sem=recvs,
            device_id=device, device_id_type=MESH,
        )
        copy.start()
        return copy

    def exchange(e, ref):
        out, into = ys.at[e], yr.at[e]
        rows = pl.ds(0, 16)
        plan = (
            (out.at[1], into.at[0, pl.ds(4, 16)], up),
            (out.at[0], into.at[1, pl.ds(4, 16)], down),
            (ref.at[pl.ds(4 + 12 * c, 4), rows], ref.at[pl.ds(20 - 20 * c, 4), rows], far),
            (ref.at[pl.ds(16 - 12 * c, 4), rows], ref.at[pl.ds(20 * c, 4), rows], near),
            (out.at[1, pl.ds(13 * c, 3)], into.at[0, pl.ds(20 - 19 * c, 3)], far_up),
            (out.at[0, pl.ds(13 * c, 3)], into.at[1, pl.ds(20 - 19 * c, 3)], far_down),
            (out.at[1, pl.ds(13 - 13 * c, 3)], into.at[0, pl.ds(1 + 19 * c, 3)], near_up),
            (out.at[0, pl.ds(13 - 13 * c, 3)], into.at[1, pl.ds(1 + 19 * c, 3)], near_down),
        )
        return [
            send(src, dst, ghost_send.at[e, i], ghost_recv.at[e, i], device)
            for i, (src, dst, device) in enumerate(plan)
        ]

    def pack(e, x, own_rows):
        ys[e, 0, x] = own_rows[0:4]
        ys[e, 1, x] = own_rows[12:16]

    loads[0].wait()
    loads[1].wait()

    def prepare(x, carry):
        d = (damping[x] + (7.0 - MID)) * (2.0 / HALF)
        diag[x + 4, 0:16] = d
        pack(0, x, d)
        v = init[x + 1]
        ps[0, x] = v[0:1]
        ps[1, x] = v[15:16]
        return carry

    lax.fori_loop(0, 16, prepare, 0)
    loads[2].wait()
    loads[3].wait()
    pl.semaphore_wait(barrier, 46)
    first_sends = [
        send(ps.at[1], pr.at[0], init_send.at[0], init_recv.at[0], up),
        send(ps.at[0], pr.at[1], init_send.at[1], init_recv.at[1], down),
        send(
            init.at[pl.ds(1 + 15 * c, 1)], init.at[pl.ds(17 - 17 * c, 1)],
            init_send.at[2], init_recv.at[2], far,
        ),
    ]
    exchanges = [exchange(0, diag)]

    for copy in first_sends:
        copy.wait_recv()
    init[0] = init[0] * x_low
    init[17] = init[17] * x_high

    def first_vector(x, carry):
        halves = [init[x + 1, :, 0:128], init[x + 1, :, 128:256]]
        along_z = zsum(*halves, first[:16], last[:16])
        done = []
        for h, v in enumerate(halves):
            s = slice(128 * h, 128 * h + 128)
            low = jnp.where(top, pr[0, x, :, s] * has_low, pltpu.roll(v, 1, 0))
            high = jnp.where(bottom, pr[1, x, :, s] * has_high, pltpu.roll(v, 15, 0))
            total = along_z[h] + low + high + init[x, :, s] + init[x + 2, :, s]
            done.append(source[x, :, s] - ((damping[x, :, s] + 6.0) * v - total))
        w = jnp.concatenate(done, axis=1)
        vec[0, x + 4, 0:16] = w
        pack(1, x, w)
        return carry

    lax.fori_loop(0, 16, first_vector, 0)
    exchanges.append(exchange(1, vec.at[0]))

    def merge(e, ref, masked):
        for copy in exchanges[e]:
            copy.wait_recv()

        def ghosts(x, carry):
            tile = jnp.concatenate([yr[e, 1, x], yr[e, 0, x]], axis=0)
            if masked:
                edge = jnp.where(x < 4, x_low, jnp.where(x >= 20, x_high, 1.0))
                keep = inside * edge
                tile = tile * jnp.concatenate([keep, keep], axis=1)
            ref[x, 16:24] = tile
            return carry

        lax.fori_loop(0, 24, ghosts, 0)
        if masked:
            for x in range(4):
                ref[x, 0:16] = ref[x, 0:16] * x_low
                ref[20 + x, 0:16] = ref[20 + x, 0:16] * x_high

    merge(0, diag, False)
    for block in range(3):
        base = 4 * block
        merge(block + 1, vec.at[base], True)
        for j in range(1, 5):
            source_k = base + j - 1

            def plane(x, j=j, source_k=source_k):
                halves = [vec[source_k, x, :, 0:128], vec[source_k, x, :, 128:256]]
                along_z = zsum(*halves, first, last)
                done = []
                for h, v in enumerate(halves):
                    s = slice(128 * h, 128 * h + 128)
                    total = along_z[h] + pltpu.roll(v, 1, 0) + pltpu.roll(v, 23, 0)
                    total = total + (vec[source_k, x - 1, :, s] + vec[source_k, x + 1, :, s])
                    t = diag[x, :, s] * v - total * (2.0 / HALF)
                    done.append(0.5 * t if j == 1 else t - vec[source_k - 1, x, :, s])
                return done

            if j < 4:

                def body(x, carry, j=j, plane=plane):
                    edge = jnp.where(x < 4, x_low, jnp.where(x >= 20, x_high, 1.0))
                    keep = inside * edge
                    for h, t in enumerate(plane(x)):
                        s = slice(128 * h, 128 * h + 128)
                        vec[base + j, x, 0:16, s] = t[0:16] * edge
                        vec[base + j, x, 16:24, s] = t[16:24] * keep
                    return carry

                lax.fori_loop(j, 24 - j, body, 0)
            else:

                def body(x, carry, plane=plane):
                    done = []
                    for h, t in enumerate(plane(x + 4)):
                        s = slice(128 * h, 128 * h + 128)
                        total = PSI[4] * t[0:16]
                        for q in range(4):
                            total = total + PSI[q] * vec[base + q, x + 4, 0:16, s]
                        done.append(total)
                    total = jnp.concatenate(done, axis=1)
                    vec[base + 4, x + 4, 0:16] = total
                    if block < 2:
                        pack(block + 2, x, total)
                    return carry

                lax.fori_loop(0, 16, body, 0)
        if block < 2:
            exchanges.append(exchange(block + 2, vec.at[base + 4]))

        def products(x, carry):
            new = []
            for h in range(4):
                at = (x + 4, slice(8 * (h // 2), 8 * (h // 2) + 8), slice(128 * (h % 2), 128 * (h % 2) + 128))
                v = [vec[(base + q,) + at] for q in range(5)]
                terms = [v[0] * v[q] for q in range(4)] + [v[4] * v[q] for q in range(4)]
                new = [n + t for n, t in zip(new, terms)] if new else terms
            return tuple(a + n for a, n in zip(carry, new))

        totals = lax.fori_loop(0, 16, products, (jnp.zeros((8, 128), F32),) * 8)
        for q, total in enumerate(totals):
            sums[8 * block + q : 8 * block + q + 1] = jnp.sum(total, axis=0, keepdims=True)

    diagonal = lax.broadcasted_iota(jnp.int32, (24, 128), 0) == lane

    def to_row(v):
        return jnp.sum(jnp.where(diagonal, v, 0.0), axis=0, keepdims=True)

    part_a[plane_slot] = to_row(jnp.sum(sums[...], axis=1, keepdims=True))

    def plane_copy(k):
        slot, device = plane_mate(k)
        return slot, pltpu.make_async_remote_copy(
            src_ref=part_a.at[plane_slot], dst_ref=part_a.at[plane_slot],
            send_sem=a_send.at[slot], recv_sem=a_recv.at[plane_slot],
            device_id=device, device_id_type=MESH,
        )

    def plane_wait(k):
        slot, device = plane_mate(k)
        return pltpu.make_async_remote_copy(
            src_ref=part_a.at[slot], dst_ref=part_a.at[slot],
            send_sem=a_send.at[slot], recv_sem=a_recv.at[slot],
            device_id=device, device_id_type=MESH,
        )

    def start_plane(k, carry):
        plane_copy(k)[1].start()
        return carry

    def finish_plane(k, carry):
        plane_wait(k).wait_recv()
        return carry

    lax.fori_loop(1, 32, start_plane, 0)
    lax.fori_loop(1, 32, finish_plane, 0)
    part_b[z] = jnp.sum(part_a[...], axis=0)
    line = []
    for k in range(1, 8):
        slot, device = line_mate(k)
        copy = pltpu.make_async_remote_copy(
            src_ref=part_b.at[z], dst_ref=part_b.at[z],
            send_sem=b_send.at[slot], recv_sem=b_recv.at[z],
            device_id=device, device_id_type=MESH,
        )
        copy.start()
        line.append((slot, device))
    for slot, device in line:
        pltpu.make_async_remote_copy(
            src_ref=part_b.at[slot], dst_ref=part_b.at[slot],
            send_sem=b_send.at[slot], recv_sem=b_recv.at[slot],
            device_id=device, device_id_type=MESH,
        ).wait_recv()
    total = jnp.sum(part_b[...], axis=0)
    nu = jnp.sum(jnp.where(diagonal, total, 0.0), axis=1, keepdims=True)
    predicted, corrected = recurrences(jnp.broadcast_to(nu, (24, 128)))

    upper = jnp.where(c == 1, 1.0, 0.0).astype(F32)
    away = [corrected[k : k + 1] + upper * (predicted[k : k + 1] - corrected[k : k + 1]) for k in range(12)]
    home = [predicted[k : k + 1] + upper * (corrected[k : k + 1] - predicted[k : k + 1]) for k in range(12)]

    def combine(ref, weights):
        def body(x, carry):
            for h in range(2):
                s = slice(128 * h, 128 * h + 128)
                acc = weights[0] * vec[0, x + 4, 0:16, s]
                for k in range(1, 12):
                    acc = acc + weights[k] * vec[k, x + 4, 0:16, s]
                ref[x, :, s] = init[x + 1, :, s] + acc
            return carry

        lax.fori_loop(0, 16, body, 0)

    combine(theirs, away)
    give = send(theirs, out_hbm.at[0, own], out_send, out_recv, near)
    combine(mine, home)
    keep_mine = pltpu.make_async_copy(mine, out_hbm.at[0, own], out_sem)
    keep_mine.start()

    for copy in first_sends:
        copy.wait_send()
    for group in exchanges:
        for copy in group:
            copy.wait_send()

    def drain(k, carry):
        plane_wait(k).wait_send()
        return carry

    lax.fori_loop(1, 32, drain, 0)
    for slot, device in line:
        pltpu.make_async_remote_copy(
            src_ref=part_b.at[z], dst_ref=part_b.at[z],
            send_sem=b_send.at[slot], recv_sem=b_recv.at[slot],
            device_id=device, device_id_type=MESH,
        ).wait_send()
    give.wait_send()
    keep_mine.wait()
    pltpu.make_async_remote_copy(
        src_ref=theirs, dst_ref=out_hbm.at[0, pl.ds(other * 16, 16)],
        send_sem=out_send, recv_sem=out_recv, device_id=near, device_id_type=MESH,
    ).wait_recv()


def per_device(init_field, source, damping):
    anywhere = pl.BlockSpec(memory_space=pl.ANY)
    dma = pltpu.SemaphoreType.DMA
    return pl.pallas_call(
        kernel,
        out_shape=jax.ShapeDtypeStruct((1, 32, 16, 256), F32),
        in_specs=[anywhere] * 3,
        out_specs=anywhere,
        scratch_shapes=[
            pltpu.VMEM((13, 24, 24, 256), F32),
            pltpu.VMEM((24, 24, 256), F32),
            pltpu.VMEM((18, 16, 256), F32),
            pltpu.VMEM((16, 16, 256), F32),
            pltpu.VMEM((16, 16, 256), F32),
            pltpu.VMEM((4, 2, 16, 4, 256), F32),
            pltpu.VMEM((4, 2, 24, 4, 256), F32),
            pltpu.VMEM((2, 16, 1, 256), F32),
            pltpu.VMEM((2, 16, 1, 256), F32),
            pltpu.VMEM((24, 128), F32),
            pltpu.VMEM((32, 1, 128), F32),
            pltpu.VMEM((8, 1, 128), F32),
            pltpu.VMEM((16, 16, 256), F32),
            pltpu.VMEM((16, 16, 256), F32),
            dma((4,)), dma((3,)), dma((3,)), dma((4, 8)), dma((4, 8)),
            dma((32,)), dma((32,)), dma((8,)), dma((8,)), dma, dma, dma,
        ],
        compiler_params=pltpu.CompilerParams(collective_id=0, has_side_effects=True),
        cost_estimate=pl.CostEstimate(flops=50_000_000, bytes_accessed=3_000_000, transcendentals=0),
    )(init_field, source, damping)


def solution(mesh):
    block = P("gx", "yz", None)
    return jax.shard_map(
        per_device,
        mesh=mesh,
        in_specs=(block, block, block),
        out_specs=P("level", "gx", "yz", None),
        check_vma=False,
    )
```

time: 820 us -> 69.7 us (0.09)
  the two profiles are of different devices: /device:TPU:40 before, /device:TPU:1 now
where the time goes in v1:
time: 69.7 us; the launch traced here: 69.5 us
  Pallas kernels  67.6 us (97%)
  local copies, waits for them, and re-layouts  1.87 us (3%)
    pallas_call x1, Pallas kernels, per_device(): pl.pallas_call(kernel, out_shape=jax.ShapeDtypeStruct((1, 32, 16, 256), F...  67.6 us
    unnamed x1, local copies, waits for them, and re-layouts  1.87 us

profile of v1, /device:TPU:1, one launch (start us, length us, event | category | flops | bytes accessed | tf_op | source)
XLA Modules:
  0.0 69.5 jit_solution(5506523361065456961)
XLA Ops:
  0.0 67.6 %shard_map.37 = f32[1,32,16,256]{3,2,1,0:T(8,128)} custom-call(f32[32,16,256]{2,1,0:T(8,128)} %init_hbm.1, f32[32,16,256]{2,1,0:T(8,128)} %source_hbm.1, f32[32,16,256]{2,1,0:T(8,128)} %damping_hbm.1), custom_call_target="tpu_custom_call" | custom-call | flops 50000000 | bytes 3000000 | tf_op jit(solution)/shard_map/pallas_call | solution.py:442
  67.6 1.9 %copy.5 = f32[1,32,16,256]{3,2,1,0:T(8,128)} copy(f32[1,32,16,256]{3,2,1,0:T(8,128)} %shard_map.37) | data formatting | bytes 1048576

commit v2 on v1

v2 whole, which is shorter than its diff:
```python
import functools

import jax
import jax.numpy as jnp
import numpy as np
from jax import lax
from jax.experimental import pallas as pl
from jax.experimental.pallas import tpu as pltpu
from jax.sharding import PartitionSpec as P

STEPS = 3
ITERS = 3
MESH = pl.DeviceIdType.MESH
F32 = jnp.float32

LOW, HIGH = 1.05, 15.0
MID, HALF = (LOW + HIGH) / 2, (HIGH - LOW) / 2
W = 4


def block_polynomial():
    cheb = np.polynomial.chebyshev
    low, high = 2.0, 13.5

    def third(lam):
        x = (lam - (low + high) / 2) / ((high - low) / 2)
        return 4 * x**3 - 3 * x

    nodes = np.cos(np.pi * (np.arange(4) + 0.5) / 4)
    lam = MID + HALF * nodes
    rho = cheb.chebfit(nodes, (1 + (lam - 1) * third(lam) / third(0.0)) / lam, 3)
    return [float(c) for c in cheb.chebmul(rho, [0.0, 1.0])]


PSI = block_polynomial()


def planes(start, count, step, body):
    def turn(i, carry):
        for u in range(step):
            body(start + i * step + u)
        return carry

    lax.fori_loop(0, count // step, turn, 0)


def zsum(v0, v1, first, last):
    a0, a1 = pltpu.roll(v0, 1, 1), pltpu.roll(v1, 1, 1)
    b0, b1 = pltpu.roll(v0, 127, 1), pltpu.roll(v1, 127, 1)
    n0 = jnp.where(first, 0.0, a0) + jnp.where(last, b1, b0)
    n1 = jnp.where(first, a0, a1) + jnp.where(last, 0.0, b1)
    return n0, n1


def recurrences(nu):
    c0, c1, c2, c3, c4 = PSI

    def pattern(rows, values):
        j = lax.rem(lax.broadcasted_iota(jnp.int32, (rows, 128), 0), 4)
        out = jnp.full((rows, 128), values[3], F32)
        for q in range(3):
            out = jnp.where(j == q, values[q], out)
        return out

    bands = {
        1: (1.0, 0.5, 0.5, 0.5 / c4),
        -1: (0.0, 0.5, 0.5, 0.5 - 0.5 * c2 / c4),
        0: (0.0, 0.0, 0.0, -0.5 * c3 / c4),
        -2: (0.0, 0.0, 0.0, -0.5 * c1 / c4),
        -3: (0.0, 0.0, 0.0, -0.5 * c0 / c4),
    }
    long = {o: pattern(24, v) for o, v in bands.items()}
    short = {o: pattern(16, v) for o, v in bands.items()}

    def shifted(v, o):
        rows = v.shape[0]
        return v if o % rows == 0 else pltpu.roll(v, o % rows, 0)

    def times(z, shift):
        f, m = z
        fx = sum(shifted(f * short[o], o) for o in bands)
        mx = sum(long[o] * shifted(m, -o) for o in bands)
        return fx + shift * f, mx + shift * m

    def inner(y, z):
        return jnp.sum(y[0] * z[1][:16], axis=0, keepdims=True)

    def axpy(y, s, z):
        return y[0] + s * z[0], y[1] + s * z[1]

    one = jnp.where(lax.broadcasted_iota(jnp.int32, (16, 128), 0) == 0, 1.0, 0.0).astype(F32)
    start = (one, nu)

    def solve(resid, answer):
        direction = resid
        norm = inner(resid, resid)
        for step in range(ITERS):
            image = times(direction, MID / HALF)
            alpha = norm / inner(direction, image)
            answer = axpy(answer, alpha, direction) if answer else (alpha * direction[0], alpha * direction[1])
            if step + 1 < ITERS:
                resid = axpy(resid, -alpha, image)
                following = inner(resid, resid)
                direction = axpy(resid, following / norm, direction)
                norm = following
        return answer

    back = (MID - 1.0) / HALF
    states = [None]
    corrected = None
    for step in range(STEPS):
        state = states[-1]
        resid = axpy(start, -1.0, times(state, back)) if state else start
        states.append(solve(resid, state))
        change = axpy(states[-1], -1.0, state) if state else states[-1]
        inside = axpy(corrected, -0.5, change) if corrected else (-0.5 * change[0], -0.5 * change[1])
        resid = axpy(start, -1.0, times(inside, back))
        corrected = solve(resid, corrected)
    return states[-1][0] * (1.0 / HALF), corrected[0] * (1.0 / HALF)


def kernel(
    init_hbm, source_hbm, damping_hbm, out_hbm,
    vec, diag, init, source, damping, ys, yr, ps, pr, sums, part_a, part_b, mine, theirs,
    local_sem, init_send, init_recv, ghost_send, ghost_recv,
    a_send, a_recv, b_send, b_recv, out_sem, out_send, out_recv,
):
    c = lax.axis_index("level")
    gx = lax.axis_index("gx")
    yz = lax.axis_index("yz")
    other = 1 - c
    beyond = lax.rem(gx + 2 * c + 3, 4)
    above, below = lax.rem(yz + 1, 32), lax.rem(yz + 31, 32)
    far, near = (other, beyond, yz), (other, gx, yz)
    up, down = (c, gx, above), (c, gx, below)
    far_up, far_down = (other, beyond, above), (other, beyond, below)
    near_up, near_down = (other, gx, above), (other, gx, below)
    neighbours = (far, near, up, down, far_up, far_down, near_up, near_down)
    y, z = lax.rem(yz, 4), lax.div(yz, 4)
    plane_slot = gx * 8 + c * 4 + y

    def plane_mate(k):
        slot = lax.rem(plane_slot + k, 32)
        return slot, (lax.rem(lax.div(slot, 4), 2), lax.div(slot, 8), z * 4 + lax.rem(slot, 4))

    def line_mate(k):
        slot = lax.rem(z + k, 8)
        return slot, (c, gx, slot * 4 + y)

    own = pl.ds(c * 16, 16)
    rows = pl.ds(8, 16)
    loads = []
    for h in range(2):
        s = pl.ds(128 * h, 128)
        loads += [
            pltpu.make_async_copy(damping_hbm.at[own, :, s], damping.at[:, h], local_sem.at[h]),
            pltpu.make_async_copy(init_hbm.at[own, :, s], init.at[pl.ds(1, 16), h, rows], local_sem.at[2 + h]),
            pltpu.make_async_copy(
                init_hbm.at[pl.ds(16 - c, 1), :, s], init.at[pl.ds(17 - 17 * c, 1), h, rows], local_sem.at[4 + h]
            ),
            pltpu.make_async_copy(source_hbm.at[own, :, s], source.at[:, h], local_sem.at[6 + h]),
        ]
    for load in loads:
        load.start()

    barrier = pltpu.get_barrier_semaphore()
    for k in range(1, 8):
        pl.semaphore_signal(barrier, inc=1, device_id=line_mate(k)[1], device_id_type=MESH)
    for device in neighbours:
        pl.semaphore_signal(barrier, inc=1, device_id=device, device_id_type=MESH)
    for k in range(1, 32):
        pl.semaphore_signal(barrier, inc=1, device_id=plane_mate(k)[1], device_id_type=MESH)

    lane = lax.broadcasted_iota(jnp.int32, (8, 128), 1)
    sublane = lax.broadcasted_iota(jnp.int32, (8, 128), 0)
    first, last = lane == 0, lane == 127
    has_low = jnp.where(yz > 0, 1.0, 0.0).astype(F32)
    has_high = jnp.where(yz < 31, 1.0, 0.0).astype(F32)
    x_low = jnp.where(gx + c > 0, 1.0, 0.0).astype(F32)
    x_high = jnp.where(gx + c < 4, 1.0, 0.0).astype(F32)

    def edge_of(x):
        return jnp.where(x < 4, x_low, jnp.where(x >= 20, x_high, 1.0))

    flying = []

    def remote(src, dst, sends, recvs, device):
        return pltpu.make_async_remote_copy(
            src_ref=src, dst_ref=dst, send_sem=sends, recv_sem=recvs,
            device_id=device, device_id_type=MESH,
        )

    def send(*what):
        copy = remote(*what)
        copy.start()
        flying.append(copy)
        return copy

    def exchange(e, ref):
        out, into = ys.at[e], yr.at[e]
        plan = (
            (out.at[1], into.at[0, pl.ds(4, 16)], up),
            (out.at[0], into.at[1, pl.ds(4, 16)], down),
            (ref.at[pl.ds(4 + 12 * c, 4), :, rows], ref.at[pl.ds(20 - 20 * c, 4), :, rows], far),
            (out.at[1, pl.ds(13 * c, 3)], into.at[0, pl.ds(20 - 19 * c, 3)], far_up),
            (out.at[0, pl.ds(13 * c, 3)], into.at[1, pl.ds(20 - 19 * c, 3)], far_down),
            (out.at[1, pl.ds(13 - 13 * c, 3)], into.at[0, pl.ds(1 + 19 * c, 3)], near_up),
            (out.at[0, pl.ds(13 - 13 * c, 3)], into.at[1, pl.ds(1 + 19 * c, 3)], near_down),
            (ref.at[pl.ds(16 - 12 * c, 4), :, rows], ref.at[pl.ds(20 * c, 4), :, rows], near),
        )
        return [
            remote(src, dst, ghost_send.at[e, i], ghost_recv.at[e, i], device)
            for i, (src, dst, device) in enumerate(plan)
        ]

    def launch(e, ref):
        for copy in exchange(e, ref):
            copy.start()

    for load in loads:
        load.wait()

    def prepare(x):
        for h in range(2):
            for t in range(2):
                at = pl.ds(8 * t, 8)
                d = (damping[x, h, at] + (7.0 - MID)) * (2.0 / HALF)
                diag[x + 4, h, pl.ds(8 + 8 * t, 8)] = d
                ys[0, t, x, h] = d[4 * t : 4 * t + 4]
            ps[0, x, h] = init[x + 1, h, 8:9]
            ps[1, x, h] = init[x + 1, h, 23:24]

    planes(0, 16, 4, prepare)
    pl.semaphore_wait(barrier, 46)
    first_sends = [
        send(ps.at[1], pr.at[0], init_send.at[0], init_recv.at[0], up),
        send(ps.at[0], pr.at[1], init_send.at[1], init_recv.at[1], down),
        send(
            init.at[pl.ds(1 + 15 * c, 1), :, rows], init.at[pl.ds(17 - 17 * c, 1), :, rows],
            init_send.at[2], init_recv.at[2], far,
        ),
    ]
    launch(0, diag)

    for copy in first_sends:
        copy.wait_recv()
    for h in range(2):
        init[0, h, rows] = init[0, h, rows] * x_low
        init[17, h, rows] = init[17, h, rows] * x_high

    def neighbours_of(ref, x, at):
        v = [ref[x, h, pl.ds(at, 8)] for h in range(2)]
        n = zsum(*v, first, last)
        total = []
        for h in range(2):
            along_y = ref[x, h, pl.ds(at - 1, 8)] + ref[x, h, pl.ds(at + 1, 8)]
            total.append(n[h] + (along_y + (ref[x - 1, h, pl.ds(at, 8)] + ref[x + 1, h, pl.ds(at, 8)])))
        return v, total

    def edge_rows(x):
        for h in range(2):
            init[x + 1, h, 7:8] = pr[0, x, h] * has_low
            init[x + 1, h, 24:25] = pr[1, x, h] * has_high

    planes(0, 16, 4, edge_rows)

    def first_vector(x):
        for t in range(2):
            v, total = neighbours_of(init, x + 1, 8 + 8 * t)
            for h in range(2):
                at = pl.ds(8 * t, 8)
                w = source[x, h, at] - ((damping[x, h, at] + 6.0) * v[h] - total[h])
                vec[0, x + 4, h, pl.ds(8 + 8 * t, 8)] = w
                ys[1, t, x, h] = w[4 * t : 4 * t + 4]

    planes(0, 16, 4, first_vector)
    launch(1, vec.at[0])

    def merge(e, ref, masked):
        for copy in exchange(e, ref):
            copy.wait_recv()

        def ghosts(x):
            edge = edge_of(x) if masked else None
            for h in range(2):
                low, high = yr[e, 0, x, h], yr[e, 1, x, h]
                if masked:
                    low, high = low * (has_low * edge), high * (has_high * edge)
                ref[x, h, 4:8] = low
                ref[x, h, 24:28] = high

        planes(0, 24, 4, ghosts)
        if masked:
            for x in range(4):
                for h in range(2):
                    ref[x, h, rows] = ref[x, h, rows] * x_low
                    ref[20 + x, h, rows] = ref[20 + x, h, rows] * x_high

    merge(0, diag, False)

    def block_of(block, carry):
        base = 4 * block
        merge(block + 1, vec.at[base], True)
        for j, step in ((1, 11), (2, 5), (3, 6)):
            starts = (4 + j, 12 + j, 20 - j)
            keep = []
            for at in starts:
                r = sublane + at
                keep.append(jnp.where(r < 8, has_low, jnp.where(r >= 24, has_high, 1.0)).astype(F32))

            def apply(x, j=j, starts=starts, keep=keep):
                edge = edge_of(x)
                for at, mask in zip(starts, keep):
                    v, total = neighbours_of(vec.at[base + j - 1], x, at)
                    for h in range(2):
                        t = diag[x, h, pl.ds(at, 8)] * v[h] - total[h] * (2.0 / HALF)
                        t = 0.5 * t if j == 1 else t - vec[base + j - 2, x, h, pl.ds(at, 8)]
                        vec[base + j, x, h, pl.ds(at, 8)] = t * (mask * edge)

            planes(j, 24 - 2 * j, step, apply)

        def close(x):
            for t in range(2):
                at = 8 + 8 * t
                v, total = neighbours_of(vec.at[base + 3], x + 4, at)
                for h in range(2):
                    old = [vec[base + q, x + 4, h, pl.ds(at, 8)] for q in range(3)]
                    new = diag[x + 4, h, pl.ds(at, 8)] * v[h] - total[h] * (2.0 / HALF) - old[2]
                    new = PSI[4] * new + (PSI[3] * v[h] + PSI[2] * old[2]) + (PSI[1] * old[1] + PSI[0] * old[0])
                    vec[base + 4, x + 4, h, pl.ds(at, 8)] = new
                    ys[block + 2, t, x, h] = new[4 * t : 4 * t + 4]

        planes(0, 16, 4, close)

        @pl.when(block < 2)
        def _():
            launch(block + 2, vec.at[base + 4])

        def products(i, carry):
            for u in range(4):
                for h in range(2):
                    for t in range(2):
                        v = [vec[base + q, 4 * i + u + 4, h, pl.ds(8 + 8 * t, 8)] for q in range(5)]
                        terms = [v[0] * v[q] for q in range(4)] + [v[4] * v[q] for q in range(4)]
                        carry = tuple(a + n for a, n in zip(carry, terms))
            return carry

        totals = lax.fori_loop(0, 4, products, (jnp.zeros((8, 128), F32),) * 8)
        for q, total in enumerate(totals):
            sums[block, q : q + 1] = jnp.sum(total, axis=0, keepdims=True)
        return carry

    lax.fori_loop(0, 3, block_of, 0)

    diagonal = lax.broadcasted_iota(jnp.int32, (24, 128), 0) == lax.broadcasted_iota(jnp.int32, (24, 128), 1)

    def to_row(v):
        return jnp.sum(jnp.where(diagonal, v, 0.0), axis=0, keepdims=True)

    part_a[plane_slot] = to_row(jnp.sum(jnp.concatenate([sums[0], sums[1], sums[2]], axis=0), axis=1, keepdims=True))

    def plane_copy(k):
        slot, device = plane_mate(k)
        return slot, pltpu.make_async_remote_copy(
            src_ref=part_a.at[plane_slot], dst_ref=part_a.at[plane_slot],
            send_sem=a_send.at[slot], recv_sem=a_recv.at[plane_slot],
            device_id=device, device_id_type=MESH,
        )

    def plane_wait(k):
        slot, device = plane_mate(k)
        return pltpu.make_async_remote_copy(
            src_ref=part_a.at[slot], dst_ref=part_a.at[slot],
            send_sem=a_send.at[slot], recv_sem=a_recv.at[slot],
            device_id=device, device_id_type=MESH,
        )

    def start_plane(k, carry):
        plane_copy(k)[1].start()
        return carry

    def finish_plane(k, carry):
        plane_wait(k).wait_recv()
        return carry

    lax.fori_loop(1, 32, start_plane, 0)
    lax.fori_loop(1, 32, finish_plane, 0)
    part_b[z] = jnp.sum(part_a[...], axis=0)
    line = []
    for k in range(1, 8):
        slot, device = line_mate(k)
        copy = pltpu.make_async_remote_copy(
            src_ref=part_b.at[z], dst_ref=part_b.at[z],
            send_sem=b_send.at[slot], recv_sem=b_recv.at[z],
            device_id=device, device_id_type=MESH,
        )
        copy.start()
        line.append((slot, device))
    for slot, device in line:
        pltpu.make_async_remote_copy(
            src_ref=part_b.at[slot], dst_ref=part_b.at[slot],
            send_sem=b_send.at[slot], recv_sem=b_recv.at[slot],
            device_id=device, device_id_type=MESH,
        ).wait_recv()
    total = jnp.sum(part_b[...], axis=0)
    nu = jnp.sum(jnp.where(diagonal, total, 0.0), axis=1, keepdims=True)
    predicted, corrected = recurrences(jnp.broadcast_to(nu, (24, 128)))

    upper = jnp.where(c == 1, 1.0, 0.0).astype(F32)
    away = [corrected[k : k + 1] + upper * (predicted[k : k + 1] - corrected[k : k + 1]) for k in range(12)]
    home = [predicted[k : k + 1] + upper * (corrected[k : k + 1] - predicted[k : k + 1]) for k in range(12)]

    def combine(ref, weights):
        spread = [jnp.broadcast_to(w, (8, 128)) for w in weights]

        def body(x):
            for h in range(2):
                for t in range(2):
                    at = pl.ds(8 + 8 * t, 8)
                    terms = [spread[k] * vec[k, x + 4, h, at] for k in range(12)]
                    terms.append(init[x + 1, h, at])
                    while len(terms) > 1:
                        terms = [a + b for a, b in zip(terms[::2], terms[1::2])] + terms[len(terms) & ~1 :]
                    ref[h, x, pl.ds(8 * t, 8)] = terms[0]

        planes(0, 16, 4, body)

    def place(h, part):
        return out_hbm.at[0, pl.ds(part * 16, 16), :, pl.ds(128 * h, 128)]

    combine(theirs, away)
    for h in range(2):
        send(theirs.at[h], place(h, c), out_send.at[h], out_recv.at[h], near)
    combine(mine, home)
    keeps = [pltpu.make_async_copy(mine.at[h], place(h, c), out_sem.at[h]) for h in range(2)]
    for copy in keeps:
        copy.start()

    for copy in flying:
        copy.wait_send()
    for e, ref in enumerate((diag, vec.at[0], vec.at[4], vec.at[8])):
        for copy in exchange(e, ref):
            copy.wait_send()

    def drain(k, carry):
        plane_wait(k).wait_send()
        return carry

    lax.fori_loop(1, 32, drain, 0)
    for slot, device in line:
        pltpu.make_async_remote_copy(
            src_ref=part_b.at[z], dst_ref=part_b.at[z],
            send_sem=b_send.at[slot], recv_sem=b_recv.at[slot],
            device_id=device, device_id_type=MESH,
        ).wait_send()
    for copy in keeps:
        copy.wait()
    for h in range(2):
        remote(theirs.at[h], place(h, other), out_send.at[h], out_recv.at[h], near).wait_recv()


def per_device(init_field, source, damping):
    anywhere = pl.BlockSpec(memory_space=pl.ANY)
    dma = pltpu.SemaphoreType.DMA
    return pl.pallas_call(
        kernel,
        out_shape=jax.ShapeDtypeStruct((1, 32, 16, 256), F32),
        in_specs=[anywhere] * 3,
        out_specs=anywhere,
        scratch_shapes=[
            pltpu.VMEM((13, 24, 2, 32, 128), F32),
            pltpu.VMEM((24, 2, 32, 128), F32),
            pltpu.VMEM((18, 2, 32, 128), F32),
            pltpu.VMEM((16, 2, 16, 128), F32),
            pltpu.VMEM((16, 2, 16, 128), F32),
            pltpu.VMEM((5, 2, 16, 2, 4, 128), F32),
            pltpu.VMEM((4, 2, 24, 2, 4, 128), F32),
            pltpu.VMEM((2, 16, 2, 1, 128), F32),
            pltpu.VMEM((2, 16, 2, 1, 128), F32),
            pltpu.VMEM((3, 8, 128), F32),
            pltpu.VMEM((32, 1, 128), F32),
            pltpu.VMEM((8, 1, 128), F32),
            pltpu.VMEM((2, 16, 16, 128), F32),
            pltpu.VMEM((2, 16, 16, 128), F32),
            dma((8,)), dma((3,)), dma((3,)), dma((4, 8)), dma((4, 8)),
            dma((32,)), dma((32,)), dma((8,)), dma((8,)), dma((2,)), dma((2,)), dma((2,)),
        ],
        compiler_params=pltpu.CompilerParams(collective_id=0, has_side_effects=True),
        cost_estimate=pl.CostEstimate(flops=50_000_000, bytes_accessed=3_000_000, transcendentals=0),
    )(init_field, source, damping)


def solution(mesh):
    block = P("gx", "yz", None)
    return jax.shard_map(
        per_device,
        mesh=mesh,
        in_specs=(block, block, block),
        out_specs=P("level", "gx", "yz", None),
        check_vma=False,
    )
```

time: 69.7 us -> 97.1 us (1.39)
  Pallas kernels: 67.6 us -> 95.1 us
    pallas_call x1, Pallas kernels: 67.6 us -> 95.1 us  [per_device(): pl.pallas_call(kernel, out_shape=jax.ShapeDtypeStruct((1, 32, 16, 256), F...]
where the time goes in v2:
time: 97.1 us; the launch traced here: 97 us
  Pallas kernels  95.1 us (98%)
  local copies, waits for them, and re-layouts  1.87 us (2%)
    pallas_call x1, Pallas kernels, per_device(): pl.pallas_call(kernel, out_shape=jax.ShapeDtypeStruct((1, 32, 16, 256), F...  95.1 us

profile of v2, /device:TPU:1, one launch (start us, length us, event | category | flops | bytes accessed | tf_op | source)
XLA Modules:
  0.0 97.0 jit_solution(7384303864747128351)
XLA Ops:
  0.0 95.1 %shard_map.37 = f32[1,32,16,256]{3,2,1,0:T(8,128)} custom-call(f32[32,16,256]{2,1,0:T(8,128)} %init_hbm.1, f32[32,16,256]{2,1,0:T(8,128)} %source_hbm.1, f32[32,16,256]{2,1,0:T(8,128)} %damping_hbm.1), custom_call_target="tpu_custom_call" | custom-call | flops 50000000 | bytes 3000000 | tf_op jit(solution)/shard_map/pallas_call | solution.py:465
  95.1 1.9 %copy.5 = f32[1,32,16,256]{3,2,1,0:T(8,128)} copy(f32[1,32,16,256]{3,2,1,0:T(8,128)} %shard_map.37) | data formatting | bytes 1048576

commit v3 on v2

--- a/solution.py
+++ b/solution.py
@@ -16,6 +16,7 @@
 LOW, HIGH = 1.05, 15.0
 MID, HALF = (LOW + HIGH) / 2, (HIGH - LOW) / 2
 W = 4
+STEP_PLANES = ((1, 11), (2, 10), (3, 9))
 
 
 def block_polynomial():
@@ -121,7 +122,7 @@
 
 def kernel(
     init_hbm, source_hbm, damping_hbm, out_hbm,
-    vec, diag, init, source, damping, ys, yr, ps, pr, sums, part_a, part_b, mine, theirs,
+    u0, u1, u2, u3, diag, init, source, damping, ys, yr, ps, pr, sums, part_a, part_b, mine, theirs,
     local_sem, init_send, init_recv, ghost_send, ghost_recv,
     a_send, a_recv, b_send, b_recv, out_sem, out_send, out_recv,
 ):
@@ -270,11 +271,11 @@
             for h in range(2):
                 at = pl.ds(8 * t, 8)
                 w = source[x, h, at] - ((damping[x, h, at] + 6.0) * v[h] - total[h])
-                vec[0, x + 4, h, pl.ds(8 + 8 * t, 8)] = w
+                u0[0, x + 4, h, pl.ds(8 + 8 * t, 8)] = w
                 ys[1, t, x, h] = w[4 * t : 4 * t + 4]
 
     planes(0, 16, 4, first_vector)
-    launch(1, vec.at[0])
+    launch(1, u0.at[0])
 
     def merge(e, ref, masked):
         for copy in exchange(e, ref):
@@ -299,9 +300,10 @@
     merge(0, diag, False)
 
     def block_of(block, carry):
-        base = 4 * block
-        merge(block + 1, vec.at[base], True)
-        for j, step in ((1, 11), (2, 5), (3, 6)):
+        basis = [u.at[block] for u in (u0, u1, u2, u3)]
+        following = u0.at[block + 1]
+        merge(block + 1, basis[0], True)
+        for j, step in STEP_PLANES:
             starts = (4 + j, 12 + j, 20 - j)
             keep = []
             for at in starts:
@@ -311,36 +313,42 @@
             def apply(x, j=j, starts=starts, keep=keep):
                 edge = edge_of(x)
                 for at, mask in zip(starts, keep):
-                    v, total = neighbours_of(vec.at[base + j - 1], x, at)
+                    v, total = neighbours_of(basis[j - 1], x, at)
                     for h in range(2):
                         t = diag[x, h, pl.ds(at, 8)] * v[h] - total[h] * (2.0 / HALF)
-                        t = 0.5 * t if j == 1 else t - vec[base + j - 2, x, h, pl.ds(at, 8)]
-                        vec[base + j, x, h, pl.ds(at, 8)] = t * (mask * edge)
+                        t = 0.5 * t if j == 1 else t - basis[j - 2][x, h, pl.ds(at, 8)]
+                        basis[j][x, h, pl.ds(at, 8)] = t * (mask * edge)
 
             planes(j, 24 - 2 * j, step, apply)
 
-        def close(x):
-            for t in range(2):
-                at = 8 + 8 * t
-                v, total = neighbours_of(vec.at[base + 3], x + 4, at)
-                for h in range(2):
-                    old = [vec[base + q, x + 4, h, pl.ds(at, 8)] for q in range(3)]
-                    new = diag[x + 4, h, pl.ds(at, 8)] * v[h] - total[h] * (2.0 / HALF) - old[2]
-                    new = PSI[4] * new + (PSI[3] * v[h] + PSI[2] * old[2]) + (PSI[1] * old[1] + PSI[0] * old[0])
-                    vec[base + 4, x + 4, h, pl.ds(at, 8)] = new
-                    ys[block + 2, t, x, h] = new[4 * t : 4 * t + 4]
-
-        planes(0, 16, 4, close)
+        def close(i, carry):
+            done = []
+            for u in range(8):
+                x = 8 * i + u + 4
+                for at in (8, 16):
+                    v, total = neighbours_of(basis[3], x, at)
+                    for h in range(2):
+                        old = [basis[q][x, h, pl.ds(at, 8)] for q in range(3)]
+                        new = diag[x, h, pl.ds(at, 8)] * v[h] - total[h] * (2.0 / HALF) - old[2]
+                        new = PSI[4] * new + (PSI[3] * v[h] + PSI[2] * old[2]) + (PSI[1] * old[1] + PSI[0] * old[0])
+                        done.append((x, h, at, new))
+            for x, h, at, new in done:
+                following[x, h, pl.ds(at, 8)] = new
+                t = at // 8 - 1
+                ys[block + 2, t, x - 4, h] = new[4 * t : 4 * t + 4]
+            return carry
+
+        lax.fori_loop(0, 2, close, 0)
 
         @pl.when(block < 2)
         def _():
-            launch(block + 2, vec.at[base + 4])
+            launch(block + 2, following)
 
         def products(i, carry):
             for u in range(4):
                 for h in range(2):
                     for t in range(2):
-                        v = [vec[base + q, 4 * i + u + 4, h, pl.ds(8 + 8 * t, 8)] for q in range(5)]
+                        v = [f[4 * i + u + 4, h, pl.ds(8 + 8 * t, 8)] for f in (*basis, following)]
                         terms = [v[0] * v[q] for q in range(4)] + [v[4] * v[q] for q in range(4)]
                         carry = tuple(a + n for a, n in zip(carry, terms))
             return carry
@@ -417,7 +425,7 @@
             for h in range(2):
                 for t in range(2):
                     at = pl.ds(8 + 8 * t, 8)
-                    terms = [spread[k] * vec[k, x + 4, h, at] for k in range(12)]
+                    terms = [spread[k] * (u0, u1, u2, u3)[k % 4][k // 4, x + 4, h, at] for k in range(12)]
                     terms.append(init[x + 1, h, at])
                     while len(terms) > 1:
                         terms = [a + b for a, b in zip(terms[::2], terms[1::2])] + terms[len(terms) & ~1 :]
@@ -438,7 +446,7 @@
 
     for copy in flying:
         copy.wait_send()
-    for e, ref in enumerate((diag, vec.at[0], vec.at[4], vec.at[8])):
+    for e, ref in enumerate((diag, u0.at[0], u0.at[1], u0.at[2])):
         for copy in exchange(e, ref):
             copy.wait_send()
 
@@ -468,7 +476,10 @@
         in_specs=[anywhere] * 3,
         out_specs=anywhere,
         scratch_shapes=[
-            pltpu.VMEM((13, 24, 2, 32, 128), F32),
+            pltpu.VMEM((4, 24, 2, 32, 128), F32),
+            pltpu.VMEM((3, 24, 2, 32, 128), F32),
+            pltpu.VMEM((3, 24, 2, 32, 128), F32),
+            pltpu.VMEM((3, 24, 2, 32, 128), F32),
             pltpu.VMEM((24, 2, 32, 128), F32),
             pltpu.VMEM((18, 2, 32, 128), F32),
             pltpu.VMEM((16, 2, 16, 128), F32),

time: 97.1 us -> 51.9 us (0.53)
  Pallas kernels: 95.1 us -> 49.9 us
    pallas_call x1, Pallas kernels: 95.1 us -> 49.9 us  [per_device(): pl.pallas_call(kernel, out_shape=jax.ShapeDtypeStruct((1, 32, 16, 256), F...]
where the time goes in v3:
time: 51.9 us; the launch traced here: 51.8 us
  Pallas kernels  49.9 us (96%)
  local copies, waits for them, and re-layouts  1.87 us (4%)
    pallas_call x1, Pallas kernels, per_device(): pl.pallas_call(kernel, out_shape=jax.ShapeDtypeStruct((1, 32, 16, 256), F...  49.9 us
    unnamed x1, local copies, waits for them, and re-layouts  1.87 us

profile of v3, /device:TPU:1, one launch (start us, length us, event | category | flops | bytes accessed | tf_op | source)
XLA Modules:
  0.0 51.8 jit_solution(14932286466178112543)
XLA Ops:
  0.0 49.9 %shard_map.37 = f32[1,32,16,256]{3,2,1,0:T(8,128)} custom-call(f32[32,16,256]{2,1,0:T(8,128)} %init_hbm.1, f32[32,16,256]{2,1,0:T(8,128)} %source_hbm.1, f32[32,16,256]{2,1,0:T(8,128)} %damping_hbm.1), custom_call_target="tpu_custom_call" | custom-call | flops 50000000 | bytes 3000000 | tf_op jit(solution)/shard_map/pallas_call | solution.py:473
  49.9 1.9 %copy.5 = f32[1,32,16,256]{3,2,1,0:T(8,128)} copy(f32[1,32,16,256]{3,2,1,0:T(8,128)} %shard_map.37) | data formatting | bytes 1048576

commit v4 on v3

--- a/solution.py
+++ b/solution.py
@@ -132,11 +132,11 @@
     other = 1 - c
     beyond = lax.rem(gx + 2 * c + 3, 4)
     above, below = lax.rem(yz + 1, 32), lax.rem(yz + 31, 32)
-    far, near = (other, beyond, yz), (other, gx, yz)
-    up, down = (c, gx, above), (c, gx, below)
-    far_up, far_down = (other, beyond, above), (other, beyond, below)
-    near_up, near_down = (other, gx, above), (other, gx, below)
-    neighbours = (far, near, up, down, far_up, far_down, near_up, near_down)
+    device_of = {
+        "near": (other, gx, yz), "up": (c, gx, above), "down": (c, gx, below), "far": (other, beyond, yz),
+        "near_up": (other, gx, above), "near_down": (other, gx, below),
+        "far_up": (other, beyond, above), "far_down": (other, beyond, below),
+    }
     y, z = lax.rem(yz, 4), lax.div(yz, 4)
     plane_slot = gx * 8 + c * 4 + y
 
@@ -148,6 +148,19 @@
         slot = lax.rem(z + k, 8)
         return slot, (c, gx, slot * 4 + y)
 
+    low_ok, high_ok = yz > 0, yz < 31
+    x_low_ok, x_high_ok = gx + c > 0, gx + c < 4
+    far_ok = jnp.logical_and(gx + 2 * c >= 1, gx + 2 * c <= 4)
+    exists = {
+        "near": None, "up": high_ok, "down": low_ok, "far": far_ok, "near_up": high_ok, "near_down": low_ok,
+        "far_up": jnp.logical_and(far_ok, high_ok), "far_down": jnp.logical_and(far_ok, low_ok),
+    }
+
+    def where_there(name, act):
+        if exists[name] is None:
+            act()
+        else:
+            pl.when(exists[name])(act)
     own = pl.ds(c * 16, 16)
     rows = pl.ds(8, 16)
     loads = []
@@ -167,56 +180,60 @@
     barrier = pltpu.get_barrier_semaphore()
     for k in range(1, 8):
         pl.semaphore_signal(barrier, inc=1, device_id=line_mate(k)[1], device_id_type=MESH)
-    for device in neighbours:
-        pl.semaphore_signal(barrier, inc=1, device_id=device, device_id_type=MESH)
+    greeted = 38
+    for name, there in exists.items():
+        where_there(
+            name,
+            lambda name=name: pl.semaphore_signal(barrier, inc=1, device_id=device_of[name], device_id_type=MESH),
+        )
+        greeted = greeted + (1 if there is None else there.astype(jnp.int32))
     for k in range(1, 32):
         pl.semaphore_signal(barrier, inc=1, device_id=plane_mate(k)[1], device_id_type=MESH)
 
     lane = lax.broadcasted_iota(jnp.int32, (8, 128), 1)
     sublane = lax.broadcasted_iota(jnp.int32, (8, 128), 0)
     first, last = lane == 0, lane == 127
-    has_low = jnp.where(yz > 0, 1.0, 0.0).astype(F32)
-    has_high = jnp.where(yz < 31, 1.0, 0.0).astype(F32)
-    x_low = jnp.where(gx + c > 0, 1.0, 0.0).astype(F32)
-    x_high = jnp.where(gx + c < 4, 1.0, 0.0).astype(F32)
+    has_low, has_high = low_ok.astype(F32), high_ok.astype(F32)
+    x_low, x_high = x_low_ok.astype(F32), x_high_ok.astype(F32)
 
     def edge_of(x):
         return jnp.where(x < 4, x_low, jnp.where(x >= 20, x_high, 1.0))
 
-    flying = []
-
-    def remote(src, dst, sends, recvs, device):
+    def remote(src, dst, sends, recvs, name):
         return pltpu.make_async_remote_copy(
             src_ref=src, dst_ref=dst, send_sem=sends, recv_sem=recvs,
-            device_id=device, device_id_type=MESH,
+            device_id=device_of[name], device_id_type=MESH,
         )
-
-    def send(*what):
-        copy = remote(*what)
-        copy.start()
-        flying.append(copy)
-        return copy
 
     def exchange(e, ref):
         out, into = ys.at[e], yr.at[e]
         plan = (
-            (out.at[1], into.at[0, pl.ds(4, 16)], up),
-            (out.at[0], into.at[1, pl.ds(4, 16)], down),
-            (ref.at[pl.ds(4 + 12 * c, 4), :, rows], ref.at[pl.ds(20 - 20 * c, 4), :, rows], far),
-            (out.at[1, pl.ds(13 * c, 3)], into.at[0, pl.ds(20 - 19 * c, 3)], far_up),
-            (out.at[0, pl.ds(13 * c, 3)], into.at[1, pl.ds(20 - 19 * c, 3)], far_down),
-            (out.at[1, pl.ds(13 - 13 * c, 3)], into.at[0, pl.ds(1 + 19 * c, 3)], near_up),
-            (out.at[0, pl.ds(13 - 13 * c, 3)], into.at[1, pl.ds(1 + 19 * c, 3)], near_down),
-            (ref.at[pl.ds(16 - 12 * c, 4), :, rows], ref.at[pl.ds(20 * c, 4), :, rows], near),
+            (out.at[1], into.at[0, pl.ds(4, 16)], "up"),
+            (out.at[0], into.at[1, pl.ds(4, 16)], "down"),
+            (ref.at[pl.ds(4 + 12 * c, 4), :, rows], ref.at[pl.ds(20 - 20 * c, 4), :, rows], "far"),
+            (out.at[1, pl.ds(13 * c, 3)], into.at[0, pl.ds(20 - 19 * c, 3)], "far_up"),
+            (out.at[0, pl.ds(13 * c, 3)], into.at[1, pl.ds(20 - 19 * c, 3)], "far_down"),
+            (out.at[1, pl.ds(13 - 13 * c, 3)], into.at[0, pl.ds(1 + 19 * c, 3)], "near_up"),
+            (out.at[0, pl.ds(13 - 13 * c, 3)], into.at[1, pl.ds(1 + 19 * c, 3)], "near_down"),
+            (ref.at[pl.ds(16 - 12 * c, 4), :, rows], ref.at[pl.ds(20 * c, 4), :, rows], "near"),
         )
         return [
-            remote(src, dst, ghost_send.at[e, i], ghost_recv.at[e, i], device)
-            for i, (src, dst, device) in enumerate(plan)
+            (name, remote(src, dst, ghost_send.at[e, i], ghost_recv.at[e, i], name))
+            for i, (src, dst, name) in enumerate(plan)
         ]
 
-    def launch(e, ref):
-        for copy in exchange(e, ref):
-            copy.start()
+    def launch(copies):
+        for name, copy in copies:
+            where_there(name, copy.start)
+
+    def receive(copies):
+        for name, copy in copies:
+            turned = name.replace("up", "down") if "up" in name else name.replace("down", "up")
+            where_there(turned, copy.wait_recv)
+
+    def sent(copies):
+        for name, copy in copies:
+            where_there(name, copy.wait_send)
 
     for load in loads:
         load.wait()
@@ -232,22 +249,21 @@
             ps[1, x, h] = init[x + 1, h, 23:24]
 
     planes(0, 16, 4, prepare)
-    pl.semaphore_wait(barrier, 46)
-    first_sends = [
-        send(ps.at[1], pr.at[0], init_send.at[0], init_recv.at[0], up),
-        send(ps.at[0], pr.at[1], init_send.at[1], init_recv.at[1], down),
-        send(
+    pl.semaphore_wait(barrier, greeted)
+    edges = [
+        ("up", remote(ps.at[1], pr.at[0], init_send.at[0], init_recv.at[0], "up")),
+        ("down", remote(ps.at[0], pr.at[1], init_send.at[1], init_recv.at[1], "down")),
+        ("far", remote(
             init.at[pl.ds(1 + 15 * c, 1), :, rows], init.at[pl.ds(17 - 17 * c, 1), :, rows],
-            init_send.at[2], init_recv.at[2], far,
-        ),
+            init_send.at[2], init_recv.at[2], "far",
+        )),
     ]
-    launch(0, diag)
-
-    for copy in first_sends:
-        copy.wait_recv()
+    launch(edges)
+    launch(exchange(0, diag))
+    receive(edges)
     for h in range(2):
-        init[0, h, rows] = init[0, h, rows] * x_low
-        init[17, h, rows] = init[17, h, rows] * x_high
+        init[0, h, rows] = jnp.where(x_low_ok, init[0, h, rows], 0.0)
+        init[17, h, rows] = jnp.where(x_high_ok, init[17, h, rows], 0.0)
 
     def neighbours_of(ref, x, at):
         v = [ref[x, h, pl.ds(at, 8)] for h in range(2)]
@@ -260,8 +276,8 @@
 
     def edge_rows(x):
         for h in range(2):
-            init[x + 1, h, 7:8] = pr[0, x, h] * has_low
-            init[x + 1, h, 24:25] = pr[1, x, h] * has_high
+            init[x + 1, h, 7:8] = jnp.where(low_ok, pr[0, x, h], 0.0)
+            init[x + 1, h, 24:25] = jnp.where(high_ok, pr[1, x, h], 0.0)
 
     planes(0, 16, 4, edge_rows)
 
@@ -275,34 +291,30 @@
                 ys[1, t, x, h] = w[4 * t : 4 * t + 4]
 
     planes(0, 16, 4, first_vector)
-    launch(1, u0.at[0])
-
-    def merge(e, ref, masked):
-        for copy in exchange(e, ref):
-            copy.wait_recv()
+    launch(exchange(1, u0.at[0]))
+
+    def merge(e, ref):
+        receive(exchange(e, ref))
 
         def ghosts(x):
-            edge = edge_of(x) if masked else None
+            x_in = jnp.logical_and(jnp.logical_or(x >= 4, x_low_ok), jnp.logical_or(x < 20, x_high_ok))
+            low_in, high_in = jnp.logical_and(low_ok, x_in), jnp.logical_and(high_ok, x_in)
             for h in range(2):
-                low, high = yr[e, 0, x, h], yr[e, 1, x, h]
-                if masked:
-                    low, high = low * (has_low * edge), high * (has_high * edge)
-                ref[x, h, 4:8] = low
-                ref[x, h, 24:28] = high
+                ref[x, h, 4:8] = jnp.where(low_in, yr[e, 0, x, h], 0.0)
+                ref[x, h, 24:28] = jnp.where(high_in, yr[e, 1, x, h], 0.0)
 
         planes(0, 24, 4, ghosts)
-        if masked:
-            for x in range(4):
-                for h in range(2):
-                    ref[x, h, rows] = ref[x, h, rows] * x_low
-                    ref[20 + x, h, rows] = ref[20 + x, h, rows] * x_high
-
-    merge(0, diag, False)
+        for x in range(4):
+            for h in range(2):
+                ref[x, h, rows] = jnp.where(x_low_ok, ref[x, h, rows], 0.0)
+                ref[20 + x, h, rows] = jnp.where(x_high_ok, ref[20 + x, h, rows], 0.0)
+
+    merge(0, diag)
 
     def block_of(block, carry):
         basis = [u.at[block] for u in (u0, u1, u2, u3)]
         following = u0.at[block + 1]
-        merge(block + 1, basis[0], True)
+        merge(block + 1, basis[0])
         for j, step in STEP_PLANES:
             starts = (4 + j, 12 + j, 20 - j)
             keep = []
@@ -342,7 +354,7 @@
 
         @pl.when(block < 2)
         def _():
-            launch(block + 2, following)
+            launch(exchange(block + 2, following))
 
         def products(i, carry):
             for u in range(4):
@@ -437,18 +449,19 @@
         return out_hbm.at[0, pl.ds(part * 16, 16), :, pl.ds(128 * h, 128)]
 
     combine(theirs, away)
-    for h in range(2):
-        send(theirs.at[h], place(h, c), out_send.at[h], out_recv.at[h], near)
+    gifts = [remote(theirs.at[h], place(h, c), out_send.at[h], out_recv.at[h], "near") for h in range(2)]
+    for copy in gifts:
+        copy.start()
     combine(mine, home)
     keeps = [pltpu.make_async_copy(mine.at[h], place(h, c), out_sem.at[h]) for h in range(2)]
     for copy in keeps:
         copy.start()
 
-    for copy in flying:
+    sent(edges)
+    for e, ref in enumerate((diag, u0.at[0], u0.at[1], u0.at[2])):
+        sent(exchange(e, ref))
+    for copy in gifts:
         copy.wait_send()
-    for e, ref in enumerate((diag, u0.at[0], u0.at[1], u0.at[2])):
-        for copy in exchange(e, ref):
-            copy.wait_send()
 
     def drain(k, carry):
         plane_wait(k).wait_send()
@@ -464,7 +477,7 @@
     for copy in keeps:
         copy.wait()
     for h in range(2):
-        remote(theirs.at[h], place(h, other), out_send.at[h], out_recv.at[h], near).wait_recv()
+        remote(theirs.at[h], place(h, other), out_send.at[h], out_recv.at[h], "near").wait_recv()
 
 
 def per_device(init_field, source, damping):

time: 51.9 us -> 51.8 us (level)
  no operation moved by 1% of the time
where the time goes in v4:
time: 51.8 us; the launch traced here: 51.6 us
  Pallas kernels  49.8 us (96%)
  local copies, waits for them, and re-layouts  1.87 us (4%)
    pallas_call x1, Pallas kernels, per_device(): pl.pallas_call(kernel, out_shape=jax.ShapeDtypeStruct((1, 32, 16, 256), F...  49.8 us
    unnamed x1, local copies, waits for them, and re-layouts  1.87 us

profile of v4, /device:TPU:1, one launch (start us, length us, event | category | flops | bytes accessed | tf_op | source)
XLA Modules:
  0.0 51.6 jit_solution(11460882652418835106)
XLA Ops:
  0.0 49.8 %shard_map.37 = f32[1,32,16,256]{3,2,1,0:T(8,128)} custom-call(f32[32,16,256]{2,1,0:T(8,128)} %init_hbm.1, f32[32,16,256]{2,1,0:T(8,128)} %source_hbm.1, f32[32,16,256]{2,1,0:T(8,128)} %damping_hbm.1), custom_call_target="tpu_custom_call" | custom-call | flops 50000000 | bytes 3000000 | tf_op jit(solution)/shard_map/pallas_call | solution.py:486
  49.8 1.9 %copy.5 = f32[1,32,16,256]{3,2,1,0:T(8,128)} copy(f32[1,32,16,256]{3,2,1,0:T(8,128)} %shard_map.37) | data formatting | bytes 1048576

commit v5 on v4

--- a/solution.py
+++ b/solution.py
@@ -16,7 +16,7 @@
 LOW, HIGH = 1.05, 15.0
 MID, HALF = (LOW + HIGH) / 2, (HIGH - LOW) / 2
 W = 4
-STEP_PLANES = ((1, 11), (2, 10), (3, 9))
+STEP_PLANES = ((1, 22), (2, 20), (3, 18))
 
 
 def block_polynomial():
@@ -43,6 +43,12 @@
         return carry
 
     lax.fori_loop(0, count // step, turn, 0)
+
+
+def tree(terms):
+    while len(terms) > 1:
+        terms = [a + b for a, b in zip(terms[::2], terms[1::2])] + terms[len(terms) & ~1 :]
+    return terms[0]
 
 
 def zsum(v0, v1, first, last):
@@ -140,13 +146,14 @@
     y, z = lax.rem(yz, 4), lax.div(yz, 4)
     plane_slot = gx * 8 + c * 4 + y
 
-    def plane_mate(k):
-        slot = lax.rem(plane_slot + k, 32)
-        return slot, (lax.rem(lax.div(slot, 4), 2), lax.div(slot, 8), z * 4 + lax.rem(slot, 4))
-
-    def line_mate(k):
-        slot = lax.rem(z + k, 8)
-        return slot, (c, gx, slot * 4 + y)
+    plane_mates = [
+        (cc, xx, z * 4 + yy)
+        for i, xx in enumerate([gx] + [lax.rem(gx + k, 4) for k in range(1, 4)])
+        for j, cc in enumerate([c, other])
+        for m, yy in enumerate([y] + [lax.rem(y + k, 4) for k in range(1, 4)])
+        if i + j + m > 0
+    ]
+    line_mates = [(c, gx, lax.rem(z + k, 8) * 4 + y) for k in range(1, 8)]
 
     low_ok, high_ok = yz > 0, yz < 31
     x_low_ok, x_high_ok = gx + c > 0, gx + c < 4
@@ -178,17 +185,21 @@
         load.start()
 
     barrier = pltpu.get_barrier_semaphore()
-    for k in range(1, 8):
-        pl.semaphore_signal(barrier, inc=1, device_id=line_mate(k)[1], device_id_type=MESH)
+
+    def greet(device):
+        pl.semaphore_signal(barrier, inc=1, device_id=device, device_id_type=MESH)
+
+    for device in line_mates:
+        greet(device)
     greeted = 38
     for name, there in exists.items():
         where_there(
             name,
-            lambda name=name: pl.semaphore_signal(barrier, inc=1, device_id=device_of[name], device_id_type=MESH),
+            functools.partial(greet, device_of[name]),
         )
         greeted = greeted + (1 if there is None else there.astype(jnp.int32))
-    for k in range(1, 32):
-        pl.semaphore_signal(barrier, inc=1, device_id=plane_mate(k)[1], device_id_type=MESH)
+    for device in plane_mates:
+        greet(device)
 
     lane = lax.broadcasted_iota(jnp.int32, (8, 128), 1)
     sublane = lax.broadcasted_iota(jnp.int32, (8, 128), 0)
@@ -206,15 +217,15 @@
         )
 
     def exchange(e, ref):
-        out, into = ys.at[e], yr.at[e]
+        slab, into = ys.at[e], yr.at[e]
         plan = (
-            (out.at[1], into.at[0, pl.ds(4, 16)], "up"),
-            (out.at[0], into.at[1, pl.ds(4, 16)], "down"),
+            (slab.at[1], into.at[0, pl.ds(4, 16)], "up"),
+            (slab.at[0], into.at[1, pl.ds(4, 16)], "down"),
             (ref.at[pl.ds(4 + 12 * c, 4), :, rows], ref.at[pl.ds(20 - 20 * c, 4), :, rows], "far"),
-            (out.at[1, pl.ds(13 * c, 3)], into.at[0, pl.ds(20 - 19 * c, 3)], "far_up"),
-            (out.at[0, pl.ds(13 * c, 3)], into.at[1, pl.ds(20 - 19 * c, 3)], "far_down"),
-            (out.at[1, pl.ds(13 - 13 * c, 3)], into.at[0, pl.ds(1 + 19 * c, 3)], "near_up"),
-            (out.at[0, pl.ds(13 - 13 * c, 3)], into.at[1, pl.ds(1 + 19 * c, 3)], "near_down"),
+            (slab.at[1, pl.ds(13 * c, 3)], into.at[0, pl.ds(20 - 19 * c, 3)], "far_up"),
+            (slab.at[0, pl.ds(13 * c, 3)], into.at[1, pl.ds(20 - 19 * c, 3)], "far_down"),
+            (slab.at[1, pl.ds(13 - 13 * c, 3)], into.at[0, pl.ds(1 + 19 * c, 3)], "near_up"),
+            (slab.at[0, pl.ds(13 - 13 * c, 3)], into.at[1, pl.ds(1 + 19 * c, 3)], "near_down"),
             (ref.at[pl.ds(16 - 12 * c, 4), :, rows], ref.at[pl.ds(20 * c, 4), :, rows], "near"),
         )
         return [
@@ -335,8 +346,8 @@
 
         def close(i, carry):
             done = []
-            for u in range(8):
-                x = 8 * i + u + 4
+            for u in range(16):
+                x = 16 * i + u + 4
                 for at in (8, 16):
                     v, total = neighbours_of(basis[3], x, at)
                     for h in range(2):
@@ -350,20 +361,22 @@
                 ys[block + 2, t, x - 4, h] = new[4 * t : 4 * t + 4]
             return carry
 
-        lax.fori_loop(0, 2, close, 0)
+        lax.fori_loop(0, 1, close, 0)
 
         @pl.when(block < 2)
         def _():
             launch(exchange(block + 2, following))
 
         def products(i, carry):
+            gathered = [[] for _ in range(8)]
             for u in range(4):
                 for h in range(2):
                     for t in range(2):
                         v = [f[4 * i + u + 4, h, pl.ds(8 + 8 * t, 8)] for f in (*basis, following)]
-                        terms = [v[0] * v[q] for q in range(4)] + [v[4] * v[q] for q in range(4)]
-                        carry = tuple(a + n for a, n in zip(carry, terms))
-            return carry
+                        for q in range(4):
+                            gathered[q].append(v[0] * v[q])
+                            gathered[4 + q].append(v[4] * v[q])
+            return tuple(a + tree(terms) for a, terms in zip(carry, gathered))
 
         totals = lax.fori_loop(0, 4, products, (jnp.zeros((8, 128), F32),) * 8)
         for q, total in enumerate(totals):
@@ -379,49 +392,22 @@
 
     part_a[plane_slot] = to_row(jnp.sum(jnp.concatenate([sums[0], sums[1], sums[2]], axis=0), axis=1, keepdims=True))
 
-    def plane_copy(k):
-        slot, device = plane_mate(k)
-        return slot, pltpu.make_async_remote_copy(
-            src_ref=part_a.at[plane_slot], dst_ref=part_a.at[plane_slot],
-            send_sem=a_send.at[slot], recv_sem=a_recv.at[plane_slot],
-            device_id=device, device_id_type=MESH,
-        )
-
-    def plane_wait(k):
-        slot, device = plane_mate(k)
-        return pltpu.make_async_remote_copy(
-            src_ref=part_a.at[slot], dst_ref=part_a.at[slot],
-            send_sem=a_send.at[slot], recv_sem=a_recv.at[slot],
-            device_id=device, device_id_type=MESH,
-        )
-
-    def start_plane(k, carry):
-        plane_copy(k)[1].start()
-        return carry
-
-    def finish_plane(k, carry):
-        plane_wait(k).wait_recv()
-        return carry
-
-    lax.fori_loop(1, 32, start_plane, 0)
-    lax.fori_loop(1, 32, finish_plane, 0)
+    def share(part, slot, sends, recvs, devices):
+        for device in devices:
+            pltpu.make_async_remote_copy(
+                src_ref=part.at[slot], dst_ref=part.at[slot], send_sem=sends, recv_sem=recvs,
+                device_id=device, device_id_type=MESH,
+            ).start()
+
+    def settle(part, sem):
+        rest = part.at[pl.ds(0, part.shape[0] - 1)]
+        pltpu.make_async_copy(rest, rest, sem).wait()
+
+    share(part_a, plane_slot, a_send, a_recv, plane_mates)
+    settle(part_a, a_recv)
     part_b[z] = jnp.sum(part_a[...], axis=0)
-    line = []
-    for k in range(1, 8):
-        slot, device = line_mate(k)
-        copy = pltpu.make_async_remote_copy(
-            src_ref=part_b.at[z], dst_ref=part_b.at[z],
-            send_sem=b_send.at[slot], recv_sem=b_recv.at[z],
-            device_id=device, device_id_type=MESH,
-        )
-        copy.start()
-        line.append((slot, device))
-    for slot, device in line:
-        pltpu.make_async_remote_copy(
-            src_ref=part_b.at[slot], dst_ref=part_b.at[slot],
-            send_sem=b_send.at[slot], recv_sem=b_recv.at[slot],
-            device_id=device, device_id_type=MESH,
-        ).wait_recv()
+    share(part_b, z, b_send, b_recv, line_mates)
+    settle(part_b, b_recv)
     total = jnp.sum(part_b[...], axis=0)
     nu = jnp.sum(jnp.where(diagonal, total, 0.0), axis=1, keepdims=True)
     predicted, corrected = recurrences(jnp.broadcast_to(nu, (24, 128)))
@@ -430,32 +416,30 @@
     away = [corrected[k : k + 1] + upper * (predicted[k : k + 1] - corrected[k : k + 1]) for k in range(12)]
     home = [predicted[k : k + 1] + upper * (corrected[k : k + 1] - predicted[k : k + 1]) for k in range(12)]
 
-    def combine(ref, weights):
-        spread = [jnp.broadcast_to(w, (8, 128)) for w in weights]
-
+    away = [jnp.broadcast_to(w, (8, 128)) for w in away]
+    home = [jnp.broadcast_to(w, (8, 128)) for w in home]
+
+    def combine(ref, h, weights):
         def body(x):
-            for h in range(2):
-                for t in range(2):
-                    at = pl.ds(8 + 8 * t, 8)
-                    terms = [spread[k] * (u0, u1, u2, u3)[k % 4][k // 4, x + 4, h, at] for k in range(12)]
-                    terms.append(init[x + 1, h, at])
-                    while len(terms) > 1:
-                        terms = [a + b for a, b in zip(terms[::2], terms[1::2])] + terms[len(terms) & ~1 :]
-                    ref[h, x, pl.ds(8 * t, 8)] = terms[0]
-
-        planes(0, 16, 4, body)
+            for t in range(2):
+                at = pl.ds(8 + 8 * t, 8)
+                terms = [weights[k] * (u0, u1, u2, u3)[k % 4][k // 4, x + 4, h, at] for k in range(12)]
+                ref[h, x, pl.ds(8 * t, 8)] = tree([init[x + 1, h, at]] + terms)
+
+        planes(0, 16, 8, body)
 
     def place(h, part):
         return out_hbm.at[0, pl.ds(part * 16, 16), :, pl.ds(128 * h, 128)]
 
-    combine(theirs, away)
-    gifts = [remote(theirs.at[h], place(h, c), out_send.at[h], out_recv.at[h], "near") for h in range(2)]
-    for copy in gifts:
-        copy.start()
-    combine(mine, home)
-    keeps = [pltpu.make_async_copy(mine.at[h], place(h, c), out_sem.at[h]) for h in range(2)]
-    for copy in keeps:
-        copy.start()
+    gifts, keeps = [], []
+    for h in range(2):
+        combine(theirs, h, away)
+        gifts.append(remote(theirs.at[h], place(h, c), out_send.at[h], out_recv.at[h], "near"))
+        gifts[-1].start()
+    for h in range(2):
+        combine(mine, h, home)
+        keeps.append(pltpu.make_async_copy(mine.at[h], place(h, c), out_sem.at[h]))
+        keeps[-1].start()
 
     sent(edges)
     for e, ref in enumerate((diag, u0.at[0], u0.at[1], u0.at[2])):
@@ -463,17 +447,8 @@
     for copy in gifts:
         copy.wait_send()
 
-    def drain(k, carry):
-        plane_wait(k).wait_send()
-        return carry
-
-    lax.fori_loop(1, 32, drain, 0)
-    for slot, device in line:
-        pltpu.make_async_remote_copy(
-            src_ref=part_b.at[z], dst_ref=part_b.at[z],
-            send_sem=b_send.at[slot], recv_sem=b_recv.at[slot],
-            device_id=device, device_id_type=MESH,
-        ).wait_send()
+    settle(part_a, a_send)
+    settle(part_b, b_send)
     for copy in keeps:
         copy.wait()
     for h in range(2):
@@ -507,7 +482,7 @@
             pltpu.VMEM((2, 16, 16, 128), F32),
             pltpu.VMEM((2, 16, 16, 128), F32),
             dma((8,)), dma((3,)), dma((3,)), dma((4, 8)), dma((4, 8)),
-            dma((32,)), dma((32,)), dma((8,)), dma((8,)), dma((2,)), dma((2,)), dma((2,)),
+            dma, dma, dma, dma, dma((2,)), dma((2,)), dma((2,)),
         ],
         compiler_params=pltpu.CompilerParams(collective_id=0, has_side_effects=True),
         cost_estimate=pl.CostEstimate(flops=50_000_000, bytes_accessed=3_000_000, transcendentals=0),

time: 51.8 us -> 49.4 us (0.954)
  Pallas kernels: 49.8 us -> 47.4 us
    pallas_call x1, Pallas kernels: 49.8 us -> 47.4 us  [per_device(): pl.pallas_call(kernel, out_shape=jax.ShapeDtypeStruct((1, 32, 16, 256), F...]
where the time goes in v5:
time: 49.4 us; the launch traced here: 49.3 us
  Pallas kernels  47.4 us (96%)
  local copies, waits for them, and re-layouts  1.87 us (4%)
    pallas_call x1, Pallas kernels, per_device(): pl.pallas_call(kernel, out_shape=jax.ShapeDtypeStruct((1, 32, 16, 256), F...  47.4 us
    unnamed x1, local copies, waits for them, and re-layouts  1.87 us

profile of v5, /device:TPU:1, one launch (start us, length us, event | category | flops | bytes accessed | tf_op | source)
XLA Modules:
  0.0 49.3 jit_solution(16192645287831698271)
XLA Ops:
  0.0 47.4 %shard_map.37 = f32[1,32,16,256]{3,2,1,0:T(8,128)} custom-call(f32[32,16,256]{2,1,0:T(8,128)} %init_hbm.1, f32[32,16,256]{2,1,0:T(8,128)} %source_hbm.1, f32[32,16,256]{2,1,0:T(8,128)} %damping_hbm.1), custom_call_target="tpu_custom_call" | custom-call | flops 50000000 | bytes 3000000 | tf_op jit(solution)/shard_map/pallas_call | solution.py:461
  47.4 1.9 %copy.5 = f32[1,32,16,256]{3,2,1,0:T(8,128)} copy(f32[1,32,16,256]{3,2,1,0:T(8,128)} %shard_map.37) | data formatting | bytes 1048576

commit v6 on v5

--- a/solution.py
+++ b/solution.py
@@ -168,6 +168,14 @@
             act()
         else:
             pl.when(exists[name])(act)
+    barrier = pltpu.get_barrier_semaphore()
+
+    def greet(device):
+        pl.semaphore_signal(barrier, inc=1, device_id=device, device_id_type=MESH)
+
+    for device in plane_mates:
+        greet(device)
+    greeted = 38
     own = pl.ds(c * 16, 16)
     rows = pl.ds(8, 16)
     loads = []
@@ -184,21 +192,13 @@
     for load in loads:
         load.start()
 
-    barrier = pltpu.get_barrier_semaphore()
-
-    def greet(device):
-        pl.semaphore_signal(barrier, inc=1, device_id=device, device_id_type=MESH)
-
-    for device in line_mates:
-        greet(device)
-    greeted = 38
     for name, there in exists.items():
         where_there(
             name,
             functools.partial(greet, device_of[name]),
         )
         greeted = greeted + (1 if there is None else there.astype(jnp.int32))
-    for device in plane_mates:
+    for device in line_mates:
         greet(device)
 
     lane = lax.broadcasted_iota(jnp.int32, (8, 128), 1)
@@ -259,7 +259,7 @@
             ps[0, x, h] = init[x + 1, h, 8:9]
             ps[1, x, h] = init[x + 1, h, 23:24]
 
-    planes(0, 16, 4, prepare)
+    planes(0, 16, 8, prepare)
     pl.semaphore_wait(barrier, greeted)
     edges = [
         ("up", remote(ps.at[1], pr.at[0], init_send.at[0], init_recv.at[0], "up")),
@@ -290,7 +290,7 @@
             init[x + 1, h, 7:8] = jnp.where(low_ok, pr[0, x, h], 0.0)
             init[x + 1, h, 24:25] = jnp.where(high_ok, pr[1, x, h], 0.0)
 
-    planes(0, 16, 4, edge_rows)
+    planes(0, 16, 16, edge_rows)
 
     def first_vector(x):
         for t in range(2):
@@ -301,7 +301,7 @@
                 u0[0, x + 4, h, pl.ds(8 + 8 * t, 8)] = w
                 ys[1, t, x, h] = w[4 * t : 4 * t + 4]
 
-    planes(0, 16, 4, first_vector)
+    planes(0, 16, 16, first_vector)
     launch(exchange(1, u0.at[0]))
 
     def merge(e, ref):
@@ -314,7 +314,7 @@
                 ref[x, h, 4:8] = jnp.where(low_in, yr[e, 0, x, h], 0.0)
                 ref[x, h, 24:28] = jnp.where(high_in, yr[e, 1, x, h], 0.0)
 
-        planes(0, 24, 4, ghosts)
+        planes(0, 24, 12, ghosts)
         for x in range(4):
             for h in range(2):
                 ref[x, h, rows] = jnp.where(x_low_ok, ref[x, h, rows], 0.0)

time: 49.4 us -> 49.4 us (level)
  no operation moved by 1% of the time
where the time goes in v6:
time: 49.4 us; the launch traced here: 49.3 us
  Pallas kernels  47.4 us (96%)
  local copies, waits for them, and re-layouts  1.87 us (4%)
    pallas_call x1, Pallas kernels, per_device(): pl.pallas_call(kernel, out_shape=jax.ShapeDtypeStruct((1, 32, 16, 256), F...  47.4 us
    unnamed x1, local copies, waits for them, and re-layouts  1.87 us

profile of v6, /device:TPU:1, one launch (start us, length us, event | category | flops | bytes accessed | tf_op | source)
XLA Modules:
  0.0 49.3 jit_solution(7382001915109774841)
XLA Ops:
  0.0 47.4 %shard_map.37 = f32[1,32,16,256]{3,2,1,0:T(8,128)} custom-call(f32[32,16,256]{2,1,0:T(8,128)} %init_hbm.1, f32[32,16,256]{2,1,0:T(8,128)} %source_hbm.1, f32[32,16,256]{2,1,0:T(8,128)} %damping_hbm.1), custom_call_target="tpu_custom_call" | custom-call | flops 50000000 | bytes 3000000 | tf_op jit(solution)/shard_map/pallas_call | solution.py:461
  47.4 1.9 %copy.5 = f32[1,32,16,256]{3,2,1,0:T(8,128)} copy(f32[1,32,16,256]{3,2,1,0:T(8,128)} %shard_map.37) | data formatting | bytes 1048576

commit v7 on v6

--- a/solution.py
+++ b/solution.py
@@ -15,8 +15,9 @@
 
 LOW, HIGH = 1.05, 15.0
 MID, HALF = (LOW + HIGH) / 2, (HIGH - LOW) / 2
-W = 4
-STEP_PLANES = ((1, 22), (2, 20), (3, 18))
+W = 6
+LAST = 2 * W + 16
+WINDOWS = ((1, (3, 11, 19, 21)), (2, (4, 12, 20)), (3, (5, 13, 19)), (4, (6, 14, 18)), (5, (7, 15, 17)))
 
 
 def block_polynomial():
@@ -30,7 +31,7 @@
     nodes = np.cos(np.pi * (np.arange(4) + 0.5) / 4)
     lam = MID + HALF * nodes
     rho = cheb.chebfit(nodes, (1 + (lam - 1) * third(lam) / third(0.0)) / lam, 3)
-    return [float(c) for c in cheb.chebmul(rho, [0.0, 1.0])]
+    return [float(c) for c in cheb.chebmul(cheb.chebmul(rho, [0.0, 1.0]), [0.0, 0.0, 1.0])]
 
 
 PSI = block_polynomial()
@@ -60,22 +61,18 @@
 
 
 def recurrences(nu):
-    c0, c1, c2, c3, c4 = PSI
-
     def pattern(rows, values):
-        j = lax.rem(lax.broadcasted_iota(jnp.int32, (rows, 128), 0), 4)
-        out = jnp.full((rows, 128), values[3], F32)
-        for q in range(3):
+        j = lax.rem(lax.broadcasted_iota(jnp.int32, (rows, 128), 0), W)
+        out = jnp.full((rows, 128), values[W - 1], F32)
+        for q in range(W - 1):
             out = jnp.where(j == q, values[q], out)
         return out
 
-    bands = {
-        1: (1.0, 0.5, 0.5, 0.5 / c4),
-        -1: (0.0, 0.5, 0.5, 0.5 - 0.5 * c2 / c4),
-        0: (0.0, 0.0, 0.0, -0.5 * c3 / c4),
-        -2: (0.0, 0.0, 0.0, -0.5 * c1 / c4),
-        -3: (0.0, 0.0, 0.0, -0.5 * c0 / c4),
-    }
+    middle = W - 2
+    bands = {1: (1.0,) + (0.5,) * middle + (0.5 / PSI[W],)}
+    for o in range(-W + 1, 1):
+        closing = -0.5 * PSI[W - 1 + o] / PSI[W] + (0.5 if o == -1 else 0.0)
+        bands[o] = (0.0,) + ((0.5 if o == -1 else 0.0),) * middle + (closing,)
     long = {o: pattern(24, v) for o, v in bands.items()}
     short = {o: pattern(16, v) for o, v in bands.items()}
 
@@ -128,7 +125,7 @@
 
 def kernel(
     init_hbm, source_hbm, damping_hbm, out_hbm,
-    u0, u1, u2, u3, diag, init, source, damping, ys, yr, ps, pr, sums, part_a, part_b, mine, theirs,
+    u0, u1, u2, u3, u4, u5, diag, init, source, damping, ys, yr, ps, pr, sums, part_a, part_b, mine, theirs,
     local_sem, init_send, init_recv, ghost_send, ghost_recv,
     a_send, a_recv, b_send, b_recv, out_sem, out_send, out_recv,
 ):
@@ -208,7 +205,7 @@
     x_low, x_high = x_low_ok.astype(F32), x_high_ok.astype(F32)
 
     def edge_of(x):
-        return jnp.where(x < 4, x_low, jnp.where(x >= 20, x_high, 1.0))
+        return jnp.where(x < W, x_low, jnp.where(x >= W + 16, x_high, 1.0))
 
     def remote(src, dst, sends, recvs, name):
         return pltpu.make_async_remote_copy(
@@ -218,15 +215,16 @@
 
     def exchange(e, ref):
         slab, into = ys.at[e], yr.at[e]
+        step, top = 16 - W, 16 + W
         plan = (
-            (slab.at[1], into.at[0, pl.ds(4, 16)], "up"),
-            (slab.at[0], into.at[1, pl.ds(4, 16)], "down"),
-            (ref.at[pl.ds(4 + 12 * c, 4), :, rows], ref.at[pl.ds(20 - 20 * c, 4), :, rows], "far"),
-            (slab.at[1, pl.ds(13 * c, 3)], into.at[0, pl.ds(20 - 19 * c, 3)], "far_up"),
-            (slab.at[0, pl.ds(13 * c, 3)], into.at[1, pl.ds(20 - 19 * c, 3)], "far_down"),
-            (slab.at[1, pl.ds(13 - 13 * c, 3)], into.at[0, pl.ds(1 + 19 * c, 3)], "near_up"),
-            (slab.at[0, pl.ds(13 - 13 * c, 3)], into.at[1, pl.ds(1 + 19 * c, 3)], "near_down"),
-            (ref.at[pl.ds(16 - 12 * c, 4), :, rows], ref.at[pl.ds(20 * c, 4), :, rows], "near"),
+            (slab.at[1], into.at[0, pl.ds(W, 16)], "up"),
+            (slab.at[0], into.at[1, pl.ds(W, 16)], "down"),
+            (ref.at[pl.ds(W + step * c, W), :, rows], ref.at[pl.ds(top - top * c, W), :, rows], "far"),
+            (slab.at[1, pl.ds(11 * c, 5)], into.at[0, pl.ds(top - 21 * c, 5)], "far_up"),
+            (slab.at[0, pl.ds(11 * c, 5)], into.at[1, pl.ds(top - 21 * c, 5)], "far_down"),
+            (slab.at[1, pl.ds(11 - 11 * c, 5)], into.at[0, pl.ds(1 + 21 * c, 5)], "near_up"),
+            (slab.at[0, pl.ds(11 - 11 * c, 5)], into.at[1, pl.ds(1 + 21 * c, 5)], "near_down"),
+            (ref.at[pl.ds(16 - step * c, W), :, rows], ref.at[pl.ds(top * c, W), :, rows], "near"),
         )
         return [
             (name, remote(src, dst, ghost_send.at[e, i], ghost_recv.at[e, i], name))
@@ -246,6 +244,15 @@
         for name, copy in copies:
             where_there(name, copy.wait_send)
 
+    def pack(e, t, x, h, tile):
+        part = tile[0:6] if t == 0 else tile[2:8]
+        if h == 0:
+            ys[e, t, x, 0] = part[0:4]
+            ys[e, t, x, 1, 0:2] = part[4:6]
+        else:
+            ys[e, t, x, 1, 2:4] = part[0:2]
+            ys[e, t, x, 2] = part[2:6]
+
     for load in loads:
         load.wait()
 
@@ -254,8 +261,8 @@
             for t in range(2):
                 at = pl.ds(8 * t, 8)
                 d = (damping[x, h, at] + (7.0 - MID)) * (2.0 / HALF)
-                diag[x + 4, h, pl.ds(8 + 8 * t, 8)] = d
-                ys[0, t, x, h] = d[4 * t : 4 * t + 4]
+                diag[x + W, h, pl.ds(8 + 8 * t, 8)] = d
+                pack(0, t, x, h, d)
             ps[0, x, h] = init[x + 1, h, 8:9]
             ps[1, x, h] = init[x + 1, h, 23:24]
 
@@ -298,8 +305,8 @@
             for h in range(2):
                 at = pl.ds(8 * t, 8)
                 w = source[x, h, at] - ((damping[x, h, at] + 6.0) * v[h] - total[h])
-                u0[0, x + 4, h, pl.ds(8 + 8 * t, 8)] = w
-                ys[1, t, x, h] = w[4 * t : 4 * t + 4]
+                u0[0, x + W, h, pl.ds(8 + 8 * t, 8)] = w
+                pack(1, t, x, h, w)
 
     planes(0, 16, 16, first_vector)
     launch(exchange(1, u0.at[0]))
@@ -308,26 +315,28 @@
         receive(exchange(e, ref))
 
         def ghosts(x):
-            x_in = jnp.logical_and(jnp.logical_or(x >= 4, x_low_ok), jnp.logical_or(x < 20, x_high_ok))
-            low_in, high_in = jnp.logical_and(low_ok, x_in), jnp.logical_and(high_ok, x_in)
-            for h in range(2):
-                ref[x, h, 4:8] = jnp.where(low_in, yr[e, 0, x, h], 0.0)
-                ref[x, h, 24:28] = jnp.where(high_in, yr[e, 1, x, h], 0.0)
-
-        planes(0, 24, 12, ghosts)
-        for x in range(4):
+            x_in = jnp.logical_and(jnp.logical_or(x >= W, x_low_ok), jnp.logical_or(x < W + 16, x_high_ok))
+            for side, ok, at in ((0, low_ok, 2), (1, high_ok, 24)):
+                there = jnp.logical_and(ok, x_in)
+                group = [jnp.where(there, yr[e, side, x, g], 0.0) for g in range(3)]
+                ref[x, 0, at : at + 4] = group[0]
+                ref[x, 0, at + 4 : at + 6] = group[1][0:2]
+                ref[x, 1, at : at + 2] = group[1][2:4]
+                ref[x, 1, at + 2 : at + 6] = group[2]
+
+        planes(0, LAST, 14, ghosts)
+        for x in range(W):
             for h in range(2):
                 ref[x, h, rows] = jnp.where(x_low_ok, ref[x, h, rows], 0.0)
-                ref[20 + x, h, rows] = jnp.where(x_high_ok, ref[20 + x, h, rows], 0.0)
+                ref[W + 16 + x, h, rows] = jnp.where(x_high_ok, ref[W + 16 + x, h, rows], 0.0)
 
     merge(0, diag)
 
     def block_of(block, carry):
-        basis = [u.at[block] for u in (u0, u1, u2, u3)]
+        basis = [u.at[block] for u in (u0, u1, u2, u3, u4, u5)]
         following = u0.at[block + 1]
         merge(block + 1, basis[0])
-        for j, step in STEP_PLANES:
-            starts = (4 + j, 12 + j, 20 - j)
+        for j, starts in WINDOWS:
             keep = []
             for at in starts:
                 r = sublane + at
@@ -342,55 +351,55 @@
                         t = 0.5 * t if j == 1 else t - basis[j - 2][x, h, pl.ds(at, 8)]
                         basis[j][x, h, pl.ds(at, 8)] = t * (mask * edge)
 
-            planes(j, 24 - 2 * j, step, apply)
+            planes(j, LAST - 2 * j, LAST - 2 * j, apply)
 
         def close(i, carry):
             done = []
             for u in range(16):
-                x = 16 * i + u + 4
+                x = 16 * i + u + W
                 for at in (8, 16):
-                    v, total = neighbours_of(basis[3], x, at)
+                    v, total = neighbours_of(basis[W - 1], x, at)
                     for h in range(2):
-                        old = [basis[q][x, h, pl.ds(at, 8)] for q in range(3)]
-                        new = diag[x, h, pl.ds(at, 8)] * v[h] - total[h] * (2.0 / HALF) - old[2]
-                        new = PSI[4] * new + (PSI[3] * v[h] + PSI[2] * old[2]) + (PSI[1] * old[1] + PSI[0] * old[0])
+                        old = [basis[q][x, h, pl.ds(at, 8)] for q in range(W - 1)]
+                        new = diag[x, h, pl.ds(at, 8)] * v[h] - total[h] * (2.0 / HALF) - old[W - 2]
+                        new = tree([PSI[W] * new] + [PSI[q] * f for q, f in enumerate(old + [v[h]])])
                         done.append((x, h, at, new))
             for x, h, at, new in done:
                 following[x, h, pl.ds(at, 8)] = new
                 t = at // 8 - 1
-                ys[block + 2, t, x - 4, h] = new[4 * t : 4 * t + 4]
+                pack(block + 2, t, x - W, h, new)
             return carry
 
         lax.fori_loop(0, 1, close, 0)
 
-        @pl.when(block < 2)
+        @pl.when(block < 1)
         def _():
             launch(exchange(block + 2, following))
 
         def products(i, carry):
-            gathered = [[] for _ in range(8)]
+            gathered = [[] for _ in range(2 * W)]
             for u in range(4):
                 for h in range(2):
                     for t in range(2):
-                        v = [f[4 * i + u + 4, h, pl.ds(8 + 8 * t, 8)] for f in (*basis, following)]
-                        for q in range(4):
+                        v = [f[4 * i + u + W, h, pl.ds(8 + 8 * t, 8)] for f in (*basis, following)]
+                        for q in range(W):
                             gathered[q].append(v[0] * v[q])
-                            gathered[4 + q].append(v[4] * v[q])
+                            gathered[W + q].append(v[W] * v[q])
             return tuple(a + tree(terms) for a, terms in zip(carry, gathered))
 
-        totals = lax.fori_loop(0, 4, products, (jnp.zeros((8, 128), F32),) * 8)
+        totals = lax.fori_loop(0, 4, products, (jnp.zeros((8, 128), F32),) * (2 * W))
         for q, total in enumerate(totals):
             sums[block, q : q + 1] = jnp.sum(total, axis=0, keepdims=True)
         return carry
 
-    lax.fori_loop(0, 3, block_of, 0)
+    lax.fori_loop(0, 2, block_of, 0)
 
     diagonal = lax.broadcasted_iota(jnp.int32, (24, 128), 0) == lax.broadcasted_iota(jnp.int32, (24, 128), 1)
 
     def to_row(v):
         return jnp.sum(jnp.where(diagonal, v, 0.0), axis=0, keepdims=True)
 
-    part_a[plane_slot] = to_row(jnp.sum(jnp.concatenate([sums[0], sums[1], sums[2]], axis=0), axis=1, keepdims=True))
+    part_a[plane_slot] = to_row(jnp.sum(jnp.concatenate([sums[0, 0:12], sums[1, 0:12]], axis=0), axis=1, keepdims=True))
 
     def share(part, slot, sends, recvs, devices):
         for device in devices:
@@ -423,7 +432,7 @@
         def body(x):
             for t in range(2):
                 at = pl.ds(8 + 8 * t, 8)
-                terms = [weights[k] * (u0, u1, u2, u3)[k % 4][k // 4, x + 4, h, at] for k in range(12)]
+                terms = [weights[k] * (u0, u1, u2, u3, u4, u5)[k % W][k // W, x + W, h, at] for k in range(12)]
                 ref[h, x, pl.ds(8 * t, 8)] = tree([init[x + 1, h, at]] + terms)
 
         planes(0, 16, 8, body)
@@ -442,7 +451,7 @@
         keeps[-1].start()
 
     sent(edges)
-    for e, ref in enumerate((diag, u0.at[0], u0.at[1], u0.at[2])):
+    for e, ref in enumerate((diag, u0.at[0], u0.at[1])):
         sent(exchange(e, ref))
     for copy in gifts:
         copy.wait_send()
@@ -464,24 +473,22 @@
         in_specs=[anywhere] * 3,
         out_specs=anywhere,
         scratch_shapes=[
-            pltpu.VMEM((4, 24, 2, 32, 128), F32),
-            pltpu.VMEM((3, 24, 2, 32, 128), F32),
-            pltpu.VMEM((3, 24, 2, 32, 128), F32),
-            pltpu.VMEM((3, 24, 2, 32, 128), F32),
-            pltpu.VMEM((24, 2, 32, 128), F32),
+            pltpu.VMEM((3, LAST, 2, 32, 128), F32),
+            *[pltpu.VMEM((2, LAST, 2, 32, 128), F32)] * 5,
+            pltpu.VMEM((LAST, 2, 32, 128), F32),
             pltpu.VMEM((18, 2, 32, 128), F32),
             pltpu.VMEM((16, 2, 16, 128), F32),
             pltpu.VMEM((16, 2, 16, 128), F32),
-            pltpu.VMEM((5, 2, 16, 2, 4, 128), F32),
-            pltpu.VMEM((4, 2, 24, 2, 4, 128), F32),
+            pltpu.VMEM((4, 2, 16, 3, 4, 128), F32),
+            pltpu.VMEM((3, 2, LAST, 3, 4, 128), F32),
             pltpu.VMEM((2, 16, 2, 1, 128), F32),
             pltpu.VMEM((2, 16, 2, 1, 128), F32),
-            pltpu.VMEM((3, 8, 128), F32),
+            pltpu.VMEM((2, 16, 128), F32),
             pltpu.VMEM((32, 1, 128), F32),
             pltpu.VMEM((8, 1, 128), F32),
             pltpu.VMEM((2, 16, 16, 128), F32),
             pltpu.VMEM((2, 16, 16, 128), F32),
-            dma((8,)), dma((3,)), dma((3,)), dma((4, 8)), dma((4, 8)),
+            dma((8,)), dma((3,)), dma((3,)), dma((3, 8)), dma((3, 8)),
             dma, dma, dma, dma, dma((2,)), dma((2,)), dma((2,)),
         ],
         compiler_params=pltpu.CompilerParams(collective_id=0, has_side_effects=True),

time: 49.4 us -> 47 us (0.951)
  Pallas kernels: 47.4 us -> 44.9 us
    pallas_call x1, Pallas kernels: 47.4 us -> 44.9 us  [per_device(): pl.pallas_call(kernel, out_shape=jax.ShapeDtypeStruct((1, 32, 16, 256), F...]
where the time goes in v7:
time: 47 us; the launch traced here: 46.8 us
  Pallas kernels  44.9 us (96%)
  local copies, waits for them, and re-layouts  1.87 us (4%)
    pallas_call x1, Pallas kernels, per_device(): pl.pallas_call(kernel, out_shape=jax.ShapeDtypeStruct((1, 32, 16, 256), F...  44.9 us
    unnamed x1, local copies, waits for them, and re-layouts  1.87 us

profile of v7, /device:TPU:1, one launch (start us, length us, event | category | flops | bytes accessed | tf_op | source)
XLA Modules:
  0.0 46.8 jit_solution(9637056274071714218)
XLA Ops:
  0.0 44.9 %shard_map.37 = f32[1,32,16,256]{3,2,1,0:T(8,128)} custom-call(f32[32,16,256]{2,1,0:T(8,128)} %init_hbm.1, f32[32,16,256]{2,1,0:T(8,128)} %source_hbm.1, f32[32,16,256]{2,1,0:T(8,128)} %damping_hbm.1), custom_call_target="tpu_custom_call" | custom-call | flops 50000000 | bytes 3000000 | tf_op jit(solution)/shard_map/pallas_call | solution.py:470
  44.9 1.9 %copy.5 = f32[1,32,16,256]{3,2,1,0:T(8,128)} copy(f32[1,32,16,256]{3,2,1,0:T(8,128)} %shard_map.37) | data formatting | bytes 1048576

commit v8 on v7

--- a/solution.py
+++ b/solution.py
@@ -217,13 +217,13 @@
         slab, into = ys.at[e], yr.at[e]
         step, top = 16 - W, 16 + W
         plan = (
-            (slab.at[1], into.at[0, pl.ds(W, 16)], "up"),
-            (slab.at[0], into.at[1, pl.ds(W, 16)], "down"),
-            (ref.at[pl.ds(W + step * c, W), :, rows], ref.at[pl.ds(top - top * c, W), :, rows], "far"),
             (slab.at[1, pl.ds(11 * c, 5)], into.at[0, pl.ds(top - 21 * c, 5)], "far_up"),
             (slab.at[0, pl.ds(11 * c, 5)], into.at[1, pl.ds(top - 21 * c, 5)], "far_down"),
             (slab.at[1, pl.ds(11 - 11 * c, 5)], into.at[0, pl.ds(1 + 21 * c, 5)], "near_up"),
             (slab.at[0, pl.ds(11 - 11 * c, 5)], into.at[1, pl.ds(1 + 21 * c, 5)], "near_down"),
+            (slab.at[1], into.at[0, pl.ds(W, 16)], "up"),
+            (slab.at[0], into.at[1, pl.ds(W, 16)], "down"),
+            (ref.at[pl.ds(W + step * c, W), :, rows], ref.at[pl.ds(top - top * c, W), :, rows], "far"),
             (ref.at[pl.ds(16 - step * c, W), :, rows], ref.at[pl.ds(top * c, W), :, rows], "near"),
         )
         return [

time: 47 us -> 46.6 us (level)
  no operation moved by 1% of the time
where the time goes in v8:
time: 46.6 us; the launch traced here: 46.4 us
  Pallas kernels  44.5 us (95%)
  local copies, waits for them, and re-layouts  1.87 us (4%)
    pallas_call x1, Pallas kernels, per_device(): pl.pallas_call(kernel, out_shape=jax.ShapeDtypeStruct((1, 32, 16, 256), F...  44.5 us
    unnamed x1, local copies, waits for them, and re-layouts  1.87 us

profile of v8, /device:TPU:1, one launch (start us, length us, event | category | flops | bytes accessed | tf_op | source)
XLA Modules:
  0.0 46.4 jit_solution(6599604092269489457)
XLA Ops:
  0.0 44.5 %shard_map.37 = f32[1,32,16,256]{3,2,1,0:T(8,128)} custom-call(f32[32,16,256]{2,1,0:T(8,128)} %init_hbm.1, f32[32,16,256]{2,1,0:T(8,128)} %source_hbm.1, f32[32,16,256]{2,1,0:T(8,128)} %damping_hbm.1), custom_call_target="tpu_custom_call" | custom-call | flops 50000000 | bytes 3000000 | tf_op jit(solution)/shard_map/pallas_call | solution.py:470
  44.6 1.9 %copy.5 = f32[1,32,16,256]{3,2,1,0:T(8,128)} copy(f32[1,32,16,256]{3,2,1,0:T(8,128)} %shard_map.37) | data formatting | bytes 1048576

commit v9 on v8

--- a/solution.py
+++ b/solution.py
@@ -377,17 +377,20 @@
             launch(exchange(block + 2, following))
 
         def products(i, carry):
-            gathered = [[] for _ in range(2 * W)]
-            for u in range(4):
-                for h in range(2):
-                    for t in range(2):
-                        v = [f[4 * i + u + W, h, pl.ds(8 + 8 * t, 8)] for f in (*basis, following)]
-                        for q in range(W):
-                            gathered[q].append(v[0] * v[q])
-                            gathered[W + q].append(v[W] * v[q])
-            return tuple(a + tree(terms) for a, terms in zip(carry, gathered))
-
-        totals = lax.fori_loop(0, 4, products, (jnp.zeros((8, 128), F32),) * (2 * W))
+            for part in range(4):
+                gathered = [[] for _ in range(2 * W)]
+                for u in range(2):
+                    for h in range(2):
+                        for t in range(2):
+                            x = 8 * i + 2 * part + u + W
+                            v = [f[x, h, pl.ds(8 + 8 * t, 8)] for f in (*basis, following)]
+                            for q in range(W):
+                                gathered[q].append(v[0] * v[q])
+                                gathered[W + q].append(v[W] * v[q])
+                carry = tuple(a + tree(terms) for a, terms in zip(carry, gathered))
+            return carry
+
+        totals = lax.fori_loop(0, 2, products, (jnp.zeros((8, 128), F32),) * (2 * W))
         for q, total in enumerate(totals):
             sums[block, q : q + 1] = jnp.sum(total, axis=0, keepdims=True)
         return carry

time: 46.6 us -> 46.5 us (level)
  no operation moved by 1% of the time
where the time goes in v9:
time: 46.5 us; the launch traced here: 46.4 us
  Pallas kernels  44.5 us (96%)
  local copies, waits for them, and re-layouts  1.87 us (4%)
    pallas_call x1, Pallas kernels, per_device(): pl.pallas_call(kernel, out_shape=jax.ShapeDtypeStruct((1, 32, 16, 256), F...  44.5 us
    unnamed x1, local copies, waits for them, and re-layouts  1.87 us

profile of v9, /device:TPU:1, one launch (start us, length us, event | category | flops | bytes accessed | tf_op | source)
XLA Modules:
  0.0 46.4 jit_solution(14357946494401811439)
XLA Ops:
  0.0 44.5 %shard_map.37 = f32[1,32,16,256]{3,2,1,0:T(8,128)} custom-call(f32[32,16,256]{2,1,0:T(8,128)} %init_hbm.1, f32[32,16,256]{2,1,0:T(8,128)} %source_hbm.1, f32[32,16,256]{2,1,0:T(8,128)} %damping_hbm.1), custom_call_target="tpu_custom_call" | custom-call | flops 50000000 | bytes 3000000 | tf_op jit(solution)/shard_map/pallas_call | solution.py:473
  44.5 1.9 %copy.5 = f32[1,32,16,256]{3,2,1,0:T(8,128)} copy(f32[1,32,16,256]{3,2,1,0:T(8,128)} %shard_map.37) | data formatting | bytes 1048576
